TPU v7x, 128 devices: a whole 4x4x4 slice. The times are simulated.
128 devices in a mesh: dom: 16 (over x, y), sub: 8 (over z, core).
Axes of the slice: x: 4, y: 4, z: 4, core: 2. Of those that a mesh axis runs over, the one named last changes fastest.
Arguments:
- features: bfloat16 [131072, 602], P(('dom', 'sub')), may hold values from -6 to 6
- w_inner: bfloat16 [602, 256], replicated, may hold values from -0.25 to 0.25
- bias_inner: float32 [256], replicated, may hold values from -6 to 6
- w_outer: bfloat16 [256, 41], replicated, may hold values from -0.375 to 0.375
- bias_outer: float32 [41], replicated, may hold values from -6 to 6
- tiles: bfloat16 [1024, 32, 128, 128], P(('dom', 'sub')), may hold values from -3 to 3
- tile_col: int32 [1024, 32], P(('dom', 'sub')), may hold values from 0 to 135, as said below
- degrees: int32 [131072], P(('dom', 'sub')), may hold values from 1 to 32
- send_rows: int32 [128, 128, 128], P(('dom', 'sub')), may hold values from -1 to 1023, as said below
Outputs:
- logits: float32 [131072, 41], P(('dom', 'sub'))
Inputs may be any that keep to these rules, and one draw needn't show every extreme that they name: send_rows[e, p, s] is the row, among device e's 1024 vertices, that fills slot s of e's list for device p, or -1 for an unused slot; live slots come first and every list has 1 to 128 live slots; every sender has a full list, and in every draw some device receives full lists from all senders. tile_col[d * 8 + r, t] is the column block, in device d's column space, of tile t of row block r; the 32 column blocks of a row block are distinct.
All inputs are finite; a program needn't handle non-finite values.
Results may differ from a plain program's by a relative error of at most 0.0042.
Values may be sent and summed in bfloat16 or wider, within the bound.
No kernel may reach another device: no remote copies, remote signals or barrier semaphores. Data moves between devices by JAX's collectives and lax.ppermute only.
A program may use at most 128 MiB of HBM per device.

v0:
```python
import jax
import jax.numpy as jnp
from jax import lax
from jax.sharding import PartitionSpec as P


def deliver_inner(outgoing):
    return lax.all_to_all(outgoing, ("dom", "sub"), split_axis=0, concat_axis=0, tiled=True)


def deliver_outer(outgoing):
    return lax.all_to_all(outgoing, ("dom", "sub"), split_axis=0, concat_axis=0, tiled=True)


def aggregate(feature_rows, tiles, tile_col, send_lists, deliver):
    block_rows = tiles.shape[2]
    width = feature_rows.shape[1]
    clipped = jnp.clip(send_lists, 0, feature_rows.shape[0] - 1)
    live_slot = (send_lists >= 0)[:, :, None]
    outgoing = jnp.where(
        live_slot, jnp.take(feature_rows, clipped, axis=0), jnp.zeros((), feature_rows.dtype)
    )
    arrived = deliver(outgoing)
    columns = jnp.concatenate([feature_rows.reshape(-1, block_rows, width), arrived], axis=0)

    def rowblock(element):
        tile_set, col_set = element
        blocks = columns[col_set]
        return jnp.einsum("tij,tjw->iw", tile_set, blocks, preferred_element_type=jnp.float32)

    summed = lax.map(rowblock, (tiles, tile_col))
    return summed.reshape(feature_rows.shape[0], width)


def on_device(
    features, w_inner, bias_inner, w_outer, bias_outer, tiles, tile_col, degrees, send_rows
):
    send_lists = send_rows[0]
    classes = w_outer.shape[1]
    padded_width = 128 * ((classes + 127) // 128)
    inv_sqrt = lax.rsqrt(degrees.astype(jnp.float32))[:, None]
    projected = (jnp.dot(features, w_inner, preferred_element_type=jnp.float32) * inv_sqrt).astype(
        jnp.bfloat16
    )
    agg_inner = aggregate(projected, tiles, tile_col, send_lists, deliver_inner)
    hidden = (inv_sqrt * jax.nn.relu(inv_sqrt * agg_inner + bias_inner)).astype(jnp.bfloat16)
    w_padded = jnp.pad(w_outer, ((0, 0), (0, padded_width - classes)))
    scores = jnp.dot(hidden, w_padded, preferred_element_type=jnp.float32).astype(jnp.bfloat16)
    agg_outer = aggregate(scores, tiles, tile_col, send_lists, deliver_outer)
    return inv_sqrt * agg_outer[:, :classes] + bias_outer


def solution(mesh):
    return jax.shard_map(
        on_device,
        mesh=mesh,
        in_specs=(
            P(("dom", "sub"), None),
            P(),
            P(),
            P(),
            P(),
            P(("dom", "sub"), None, None, None),
            P(("dom", "sub"), None),
            P(("dom", "sub")),
            P(("dom", "sub"), None, None),
        ),
        out_specs=P(("dom", "sub"), None),
        check_vma=False,
    )
```

profile of v0, /device:TPU:1, one launch (start us, length us, event | category | flops | bytes accessed | tf_op | source)
XLA Modules:
  0.0 435.1 jit_solution(853206017263194829)
XLA Ops:
  0.0 1.0 fusion.18
  1.0 0.9 compare_and_fusion
  3.4 1.6 fusion.12
  5.0 65.3 %gather_fusion.2 = bf16[16384,256]{1,0:T(8,128)(2,1)} fusion(bf16[1024,256]{1,0:T(8,128)(2,1)S(1)} %fusion.12, s32[16384]{0:T(1024)S(1)} %fusion.18), kind=kCustom, calls=%fused_computation.2 | custom fusion | bytes 16842752 | tf_op jit(solution)/shard_map/jit(_take)/gather | solution.py:21
  70.3 7.7 %select_select_fusion = bf16[128,128,256]{2,1,0:T(8,128)(2,1)} fusion(bf16[128,128,256]{2,1,0:T(8,128)(2,1)} %bitcast.87, pred[128,128]{1,0:T(8,128)(4,1)S(1)} %compare_and_fusion, pred[128,128]{1,0:T(8,128)(4,1)S(1)} %compare_bitcast_fusion), kind=kLoop, calls=%fused_computation.25 | loop fusion | flops 8388608 | bytes 16809984 | tf_op jit(solution)/shard_map/jit(_where)/select_n | solution.py:20
  78.0 11.9 %all-to-all-start = ((bf16[128,128,256]{2,1,0:T(8,128)(2,1)}), bf16[128,128,256]{2,1,0:T(8,128)(2,1)}, u32[]{:S(2)}, u32[]{:S(2)}) async-start(bf16[128,128,256]{2,1,0:T(8,128)(2,1)} %select_select_fusion), calls=%async_computation | async-start | bytes 16777216 | tf_op jit(solution)/shard_map/all_to_all | solution.py:8
  89.9 98.9 %all-to-all-done = bf16[128,128,256]{2,1,0:T(8,128)(2,1)} async-done(((bf16[128,128,256]{2,1,0:T(8,128)(2,1)}), bf16[128,128,256]{2,1,0:T(8,128)(2,1)}, u32[]{:S(2)}, u32[]{:S(2)}) %all-to-all-start) | async-done | bytes 8388640 | tf_op jit(solution)/shard_map/all_to_all | solution.py:8
  188.8 7.6 %pad_maximum_fusion = bf16[136,128,256]{2,1,0:T(8,128)(2,1)} fusion(bf16[128,128,256]{2,1,0:T(8,128)(2,1)} %all-to-all-done, bf16[8,128,256]{2,1,0:T(8,128)(2,1)S(1)} %bitcast.85), kind=kLoop, calls=%fused_computation.24 | loop fusion | flops 4456448 | bytes 17825792 | tf_op jit(solution)/shard_map/concatenate | solution.py:24
  196.4 58.0 %while.20 = (s32[]{:T(128)}, f32[8,128,256]{2,1,0:T(8,128)}, bf16[8,32,128,128]{3,2,1,0:T(8,128)(2,1)}, s32[8,32]{1,0:T(8,128)}, bf16[136,128,256]{2,1,0:T(8,128)(2,1)}, /*index=5*/s32[]{:T(128)}) while((s32[]{:T(128)}, f32[8,128,256]{2,1,0:T(8,128)}, bf16[8,32,128,128]{3,2,1,0:T(8,128)(2,1)}, s32[8,32]{1,0:T(8,128)}, ...), condition=%wide.region_1.2_spmd, body=%wide.region_0.1_spmd.sunk | while | flops 268436576 | bytes 7476809 | solution.py:31
  197.1 4.2 gather_fusion
  201.3 2.3 fusion.37
  204.4 4.2 gather_fusion
  208.6 2.3 fusion.37
  211.6 4.2 gather_fusion
  215.8 2.3 fusion.37
  218.9 4.2 gather_fusion
  223.1 2.3 fusion.37
  226.1 4.2 gather_fusion
  230.3 2.3 fusion.37
  233.4 4.2 gather_fusion
  237.6 2.3 fusion.37
  240.6 4.2 gather_fusion
  244.8 2.3 fusion.37
  247.9 4.2 gather_fusion
  252.1 2.3 fusion.37
  254.4 1.4 fusion.16
  256.2 57.8 %gather_fusion.3 = bf16[16384,128]{1,0:T(8,128)(2,1)} fusion(bf16[1024,128]{1,0:T(8,128)(2,1)S(1)} %convolution_convert_fusion, s32[16384]{0:T(1024)S(1)} %fusion.18), kind=kCustom, calls=%fused_computation.3 | custom fusion | bytes 8454144 | tf_op jit(solution)/shard_map/jit(_take)/gather | solution.py:21
  314.0 7.4 %select_select_fusion.1 = bf16[128,128,128]{2,1,0:T(8,128)(2,1)} fusion(bf16[128,128,128]{2,1,0:T(8,128)(2,1)} %bitcast.88, pred[128,128]{1,0:T(8,128)(4,1)S(1)} %compare_and_fusion, pred[128,128]{1,0:T(8,128)(4,1)S(1)} %compare_bitcast_fusion), kind=kLoop, calls=%fused_computation.27 | loop fusion | flops 4194304 | bytes 8421376 | tf_op jit(solution)/shard_map/jit(_where)/select_n | solution.py:20
  321.4 11.9 %all-to-all-start.1 = ((bf16[128,128,128]{2,1,0:T(8,128)(2,1)}), bf16[128,128,128]{2,1,0:T(8,128)(2,1)}, u32[]{:S(2)}, u32[]{:S(2)}) async-start(bf16[128,128,128]{2,1,0:T(8,128)(2,1)} %select_select_fusion.1), calls=%async_computation.1 | async-start | bytes 8388608 | tf_op jit(solution)/shard_map/all_to_all | solution.py:12
  333.3 52.7 %all-to-all-done.1 = bf16[128,128,128]{2,1,0:T(8,128)(2,1)} async-done(((bf16[128,128,128]{2,1,0:T(8,128)(2,1)}), bf16[128,128,128]{2,1,0:T(8,128)(2,1)}, u32[]{:S(2)}, u32[]{:S(2)}) %all-to-all-start.1) | async-done | bytes 4194336 | tf_op jit(solution)/shard_map/all_to_all | solution.py:12
  386.0 4.6 %pad_maximum_fusion.1 = bf16[136,128,128]{2,1,0:T(8,128)(2,1)} fusion(bf16[128,128,128]{2,1,0:T(8,128)(2,1)} %all-to-all-done.1, bf16[8,128,128]{2,1,0:T(8,128)(2,1)S(1)} %bitcast.86), kind=kLoop, calls=%fused_computation.26 | loop fusion | flops 2228224 | bytes 8912896 | tf_op jit(solution)/shard_map/concatenate | solution.py:24
  390.6 43.2 %while.21 = (s32[]{:T(128)}, f32[8,128,128]{2,1,0:T(8,128)S(1)}, bf16[8,32,128,128]{3,2,1,0:T(8,128)(2,1)}, s32[8,32]{1,0:T(8,128)}, bf16[136,128,128]{2,1,0:T(8,128)(2,1)}, /*index=5*/s32[]{:T(128)}) while((s32[]{:T(128)}, f32[8,128,128]{2,1,0:T(8,128)S(1)}, bf16[8,32,128,128]{3,2,1,0:T(8,128)(2,1)}, s32[8,32]{1,0:T(8,128)}, ...), condition=%wide.region_3.4_spmd, body=%wide.region_2.3_spmd.sunk | while | flops 134218848 | bytes 4265545 | solution.py:31
  391.3 3.0 gather_fusion.1
  394.3 1.7 fusion.41
  396.7 3.0 gather_fusion.1
  399.7 1.7 fusion.41
  402.1 3.0 gather_fusion.1
  405.1 1.7 fusion.41
  407.5 3.0 gather_fusion.1
  410.5 1.7 fusion.41
  412.9 3.0 gather_fusion.1
  415.9 1.7 fusion.41
  418.2 3.0 gather_fusion.1
  421.3 1.7 fusion.41
  423.6 3.0 gather_fusion.1
  426.7 1.7 fusion.41
  429.0 3.0 gather_fusion.1
  432.1 1.7 fusion.41
  (49 shorter events, 14.5 us)
Async XLA Ops:
  0.0 3.4 copy-start
  78.0 110.8 %all-to-all-start = ((bf16[128,128,256]{2,1,0:T(8,128)(2,1)}), bf16[128,128,256]{2,1,0:T(8,128)(2,1)}, u32[]{:S(2)}, u32[]{:S(2)}) async-start(bf16[128,128,256]{2,1,0:T(8,128)(2,1)} %select_select_fusion), calls=%async_computation | async-start | bytes 16777216 | tf_op jit(solution)/shard_map/all_to_all | solution.py:8
  196.4 58.0 %copy-start.3 = (f32[256]{0:T(256)S(1)}, f32[256]{0:T(256)}, u32[]{:S(2)}) copy-start(f32[256]{0:T(256)} %param.15) | copy-start | bytes 3076
  196.4 59.5 %copy-start.2 = (bf16[256,41]{0,1:T(8,128)(2,1)S(1)}, bf16[256,41]{0,1:T(8,128)(2,1)}, u32[]{:S(2)}) copy-start(bf16[256,41]{0,1:T(8,128)(2,1)} %param.16) | copy-start | bytes 62980
  321.4 64.6 %all-to-all-start.1 = ((bf16[128,128,128]{2,1,0:T(8,128)(2,1)}), bf16[128,128,128]{2,1,0:T(8,128)(2,1)}, u32[]{:S(2)}, u32[]{:S(2)}) async-start(bf16[128,128,128]{2,1,0:T(8,128)(2,1)} %select_select_fusion.1), calls=%async_computation.1 | async-start | bytes 8388608 | tf_op jit(solution)/shard_map/all_to_all | solution.py:12
  390.6 43.4 %copy-start.4 = (f32[41]{0:T(128)S(1)}, f32[41]{0:T(128)}, u32[]{:S(2)}) copy-start(f32[41]{0:T(128)} %param.17) | copy-start | bytes 496
  433.7 1.4 copy-start.1
where the time goes:
time: 437 us; the launch traced here: 435 us
  local copies, waits for them, and re-layouts  181 us (41%)
  waiting for transfers between devices  152 us (35%)
  other arithmetic  44.1 us (10%)
  matrix products  33.7 us (8%)
  starting transfers between devices  23.8 us (5%)
    gather x2, local copies, waits for them, and re-layouts, aggregate(): jnp.take(feature_rows, clipped, axis=0)  123 us
    all_to_all x1, waiting for transfers between devices, deliver_inner(): lax.all_to_all(outgoing, ('dom', 'sub'), split_axis=0, concat_axis=0, til...  98.9 us
    gather x16, local copies, waits for them, and re-layouts, rowblock(): blocks = columns[col_set]  57.8 us
    all_to_all x1, waiting for transfers between devices, deliver_outer(): lax.all_to_all(outgoing, ('dom', 'sub'), split_axis=0, concat_axis=0, til...  52.7 us
    dot_general x16, matrix products, rowblock(): jnp.einsum('tij,tjw->iw', tile_set, blocks, preferred_element_type=jnp.fl...  31.8 us
    select_n x2, other arithmetic, aggregate(): jnp.where(live_slot, jnp.take(feature_rows, clipped, axis=0), jnp.zeros((...  15.1 us
    concatenate x2, other arithmetic, aggregate(): jnp.concatenate([feature_rows.reshape(-1, block_rows, width), arrived], a...  12.2 us
    all_to_all x1, starting transfers between devices, deliver_inner(): lax.all_to_all(outgoing, ('dom', 'sub'), split_axis=0, concat_axis=0, til...  11.9 us
  transfers between devices with their start and end apart: 2, of which 2 were waited for; matrix products, arithmetic and copies ran while one was open for 0% of the time, Pallas kernels for 0%

commit v1 on v0

v1 whole, which is shorter than its diff:
```python
import functools

import jax
import jax.numpy as jnp
from jax import lax
from jax.experimental import pallas as pl
from jax.experimental.pallas import tpu as pltpu
from jax.sharding import PartitionSpec as P

BLOCK = 128
PEER_STEP = 8


def gather_rows_kernel(lists_ref, rows_ref, out_ref):
    height = rows_ref.shape[0]
    by_slot = lists_ref[...].T
    row_of_lane = lax.broadcasted_iota(jnp.int32, (BLOCK, height), 1)
    rows = rows_ref[...]
    for p in range(PEER_STEP):
        pick = (by_slot[:, p : p + 1] == row_of_lane).astype(jnp.float32).astype(jnp.bfloat16)
        out_ref[p] = jnp.dot(pick, rows, preferred_element_type=jnp.float32).astype(jnp.bfloat16)


def gather_rows(lists, rows):
    peers = lists.shape[0]
    height, width = rows.shape
    return pl.pallas_call(
        gather_rows_kernel,
        grid=(peers // PEER_STEP,),
        in_specs=[
            pl.BlockSpec((PEER_STEP, BLOCK), lambda g: (g, 0)),
            pl.BlockSpec((height, width), lambda g: (0, 0)),
        ],
        out_specs=pl.BlockSpec((PEER_STEP, BLOCK, width), lambda g: (g, 0, 0)),
        out_shape=jax.ShapeDtypeStruct((peers, BLOCK, width), jnp.bfloat16),
        name="gather_rows",
    )(lists, rows)


def inner_kernel(
    cols_ref, tiles_ref, own_ref, arrived_ref, inv_ref, bias_ref, w_ref, out_ref, space, sems
):
    step = pl.program_id(0)
    own_blocks = own_ref.shape[0]

    @pl.when(step == 0)
    def _():
        far = pltpu.make_async_copy(arrived_ref, space.at[pl.ds(own_blocks, arrived_ref.shape[0])], sems.at[0])
        near = pltpu.make_async_copy(own_ref, space.at[pl.ds(0, own_blocks)], sems.at[1])
        far.start()
        near.start()
        near.wait()
        far.wait()

    total = jnp.zeros(space.shape[1:], jnp.float32)
    for t in range(0, tiles_ref.shape[1], 2):
        left = jnp.concatenate([tiles_ref[0, t], tiles_ref[0, t + 1]], axis=1)
        right = jnp.concatenate([space[cols_ref[step, t]], space[cols_ref[step, t + 1]]], axis=0)
        total = total + jnp.dot(left, right, preferred_element_type=jnp.float32)
    inv = inv_ref[...]
    hidden = (inv * jnp.maximum(inv * total + bias_ref[...], 0.0)).astype(jnp.bfloat16)
    out_ref[...] = lax.dot_general(
        w_ref[...], hidden, (((1,), (1,)), ((), ())), preferred_element_type=jnp.float32
    ).astype(jnp.bfloat16)


def inner_aggregate(tile_col, tiles, own, arrived, inv_col, bias, w_t):
    row_blocks, count, _, _ = tiles.shape
    width = own.shape[-1]
    peers = arrived.shape[0]
    return pl.pallas_call(
        inner_kernel,
        grid_spec=pltpu.PrefetchScalarGridSpec(
            num_scalar_prefetch=1,
            grid=(row_blocks,),
            in_specs=[
                pl.BlockSpec((1, count, BLOCK, BLOCK), lambda g, c: (g, 0, 0, 0)),
                pl.BlockSpec(memory_space=pl.ANY),
                pl.BlockSpec(memory_space=pl.ANY),
                pl.BlockSpec((BLOCK, 1), lambda g, c: (g, 0)),
                pl.BlockSpec((1, width), lambda g, c: (0, 0)),
                pl.BlockSpec(w_t.shape, lambda g, c: (0, 0)),
            ],
            out_specs=pl.BlockSpec((w_t.shape[0], BLOCK), lambda g, c: (0, g)),
            scratch_shapes=[
                pltpu.VMEM((row_blocks + peers, BLOCK, width), jnp.bfloat16),
                pltpu.SemaphoreType.DMA((2,)),
            ],
        ),
        out_shape=jax.ShapeDtypeStruct((w_t.shape[0], row_blocks * BLOCK), jnp.bfloat16),
        name="inner_aggregate",
    )(tile_col, tiles, own, arrived, inv_col, bias, w_t)


def gather_scores_kernel(lists_ref, stacked_ref, out_ref):
    quarter_rows = stacked_ref.shape[1]
    classes = out_ref.shape[1]
    stacked = stacked_ref[...]
    row_of_sublane = lax.broadcasted_iota(jnp.int32, (quarter_rows, 2 * BLOCK), 0)
    for p in range(0, PEER_STEP, 2):
        index = jnp.concatenate([lists_ref[p : p + 1], lists_ref[p + 1 : p + 2]], axis=1)
        low = jnp.bitwise_and(index, quarter_rows - 1)
        quarter = jnp.right_shift(index, quarter_rows.bit_length() - 1)
        pick = (low == row_of_sublane).astype(jnp.float32).astype(jnp.bfloat16)
        every = jnp.dot(stacked, pick, preferred_element_type=jnp.float32)
        chosen = jnp.zeros((classes, 2 * BLOCK), jnp.float32)
        for q in range(stacked_ref.shape[0] // classes):
            chosen = jnp.where(quarter == q, every[q * classes : (q + 1) * classes], chosen)
        chosen = chosen.astype(jnp.bfloat16)
        out_ref[p] = chosen[:, :BLOCK]
        out_ref[p + 1] = chosen[:, BLOCK:]


def gather_scores(lists, scores_t):
    peers = lists.shape[0]
    classes, height = scores_t.shape
    quarters = height // 256
    stacked = scores_t.reshape(classes, quarters, 256).transpose(1, 0, 2).reshape(quarters * classes, 256)
    return pl.pallas_call(
        gather_scores_kernel,
        grid=(peers // PEER_STEP,),
        in_specs=[
            pl.BlockSpec((PEER_STEP, BLOCK), lambda g: (g, 0)),
            pl.BlockSpec(stacked.shape, lambda g: (0, 0)),
        ],
        out_specs=pl.BlockSpec((PEER_STEP, classes, BLOCK), lambda g: (g, 0, 0)),
        out_shape=jax.ShapeDtypeStruct((peers, classes, BLOCK), jnp.bfloat16),
        name="gather_scores",
    )(lists, stacked)


def outer_kernel(cols_ref, tiles_ref, own_ref, arrived_ref, inv_ref, bias_ref, out_ref, space):
    step = pl.program_id(0)
    own_blocks = tiles_ref.shape[1] and own_ref.shape[1] // BLOCK

    @pl.when(step == 0)
    def _():
        for b in range(own_blocks):
            space[b] = own_ref[:, b * BLOCK : (b + 1) * BLOCK]
        space[own_blocks:] = arrived_ref[...]

    total = jnp.zeros(out_ref.shape, jnp.float32)
    for t in range(0, tiles_ref.shape[1], 2):
        right = jnp.concatenate([tiles_ref[0, t], tiles_ref[0, t + 1]], axis=1)
        left = jnp.concatenate([space[cols_ref[step, t]], space[cols_ref[step, t + 1]]], axis=1)
        total = total + lax.dot_general(
            left, right, (((1,), (1,)), ((), ())), preferred_element_type=jnp.float32
        )
    out_ref[...] = inv_ref[...] * total + bias_ref[...]


def outer_aggregate(tile_col, tiles, own_t, arrived, inv_row, bias_col):
    row_blocks, count, _, _ = tiles.shape
    classes = own_t.shape[0]
    peers = arrived.shape[0]
    return pl.pallas_call(
        outer_kernel,
        grid_spec=pltpu.PrefetchScalarGridSpec(
            num_scalar_prefetch=1,
            grid=(row_blocks,),
            in_specs=[
                pl.BlockSpec((1, count, BLOCK, BLOCK), lambda g, c: (g, 0, 0, 0)),
                pl.BlockSpec(own_t.shape, lambda g, c: (0, 0)),
                pl.BlockSpec(arrived.shape, lambda g, c: (0, 0, 0)),
                pl.BlockSpec((1, BLOCK), lambda g, c: (0, g)),
                pl.BlockSpec((classes, 1), lambda g, c: (0, 0)),
            ],
            out_specs=pl.BlockSpec((classes, BLOCK), lambda g, c: (0, g)),
            scratch_shapes=[pltpu.VMEM((row_blocks + peers, classes, BLOCK), jnp.bfloat16)],
        ),
        out_shape=jax.ShapeDtypeStruct((classes, row_blocks * BLOCK), jnp.float32),
        name="outer_aggregate",
    )(tile_col, tiles, own_t, arrived, inv_row, bias_col)


def exchange(outgoing):
    return lax.all_to_all(outgoing, ("dom", "sub"), split_axis=0, concat_axis=0, tiled=True)


def on_device(
    features, w_inner, bias_inner, w_outer, bias_outer, tiles, tile_col, degrees, send_rows
):
    lists = send_rows[0]
    classes = w_outer.shape[1]
    padded = 16 * ((classes + 15) // 16)
    width = w_inner.shape[1]
    inv_sqrt = lax.rsqrt(degrees.astype(jnp.float32))
    inv_col = inv_sqrt[:, None]
    projected = (jnp.dot(features, w_inner, preferred_element_type=jnp.float32) * inv_col).astype(
        jnp.bfloat16
    )
    arrived = exchange(gather_rows(lists, projected))
    w_t = jnp.pad(w_outer.T, ((0, padded - classes), (0, 0)))
    scores_t = inner_aggregate(
        tile_col, tiles, projected.reshape(-1, BLOCK, width), arrived, inv_col, bias_inner[None, :], w_t
    )
    arrived_scores = exchange(gather_scores(lists, scores_t))
    bias_col = jnp.pad(bias_outer, (0, padded - classes))[:, None]
    logits_t = outer_aggregate(tile_col, tiles, scores_t, arrived_scores, inv_sqrt[None, :], bias_col)
    return logits_t[:classes].T


def solution(mesh):
    return jax.shard_map(
        on_device,
        mesh=mesh,
        in_specs=(
            P(("dom", "sub"), None),
            P(),
            P(),
            P(),
            P(),
            P(("dom", "sub"), None, None, None),
            P(("dom", "sub"), None),
            P(("dom", "sub")),
            P(("dom", "sub"), None, None),
        ),
        out_specs=P(("dom", "sub"), None),
        check_vma=False,
    )
```

time: 437 us -> 208 us (0.48)
  local copies, waits for them, and re-layouts: 181 us -> 7.19 us
  Pallas kernels: 0 us -> 51.4 us
  other arithmetic: 44.1 us -> 0.79 us
  matrix products: 33.7 us -> 2.42 us
  waiting for transfers between devices: 152 us -> 121 us
    gather x18 -> x0, local copies, waits for them, and re-layouts: 181 us -> none  [the longest x2 123 us: aggregate(): jnp.take(feature_rows, clipped, axis=0)]
    pallas_call x0 -> x4, Pallas kernels: none -> 51.4 us  [the longest x1 19 us: gather_rows(): pl.pallas_call(gather_rows_kernel, grid=(peers // PEER_STEP,), in_specs=[...]
    dot_general x18 -> x1, matrix products: 33.7 us -> 2.42 us  [on_device(): jnp.dot(features, w_inner, preferred_element_type=jnp.float32) * inv_col]
    all_to_all x2, waiting for transfers between devices: 152 us -> 121 us  [exchange(): lax.all_to_all(outgoing, ('dom', 'sub'), split_axis=0, concat_axis=0, til...]
    select_n x18 -> x0, other arithmetic: 26.2 us -> none  [the longest x2 15.1 us: aggregate(): jnp.where(live_slot, jnp.take(feature_rows, clipped, axis=0), jnp.zeros((...]
    concatenate x2 -> x0, other arithmetic: 12.2 us -> none  [aggregate(): jnp.concatenate([feature_rows.reshape(-1, block_rows, width), arrived], a...]
  transfers between devices with their start and end apart: 2 -> 2, of which waited for: 2 -> 2; matrix products, arithmetic and copies ran while one was open for 0% -> 1% of each run, Pallas kernels for 0% -> 0%
where the time goes in v1:
time: 208 us; the launch traced here: 206 us
  waiting for transfers between devices  121 us (58%)
  Pallas kernels  51.4 us (25%)
  starting transfers between devices  23.3 us (11%)
  local copies, waits for them, and re-layouts  7.19 us (3%)
  matrix products  2.42 us (1%)
    all_to_all x2, waiting for transfers between devices, exchange(): lax.all_to_all(outgoing, ('dom', 'sub'), split_axis=0, concat_axis=0, til...  121 us
    all_to_all x2, starting transfers between devices, exchange(): lax.all_to_all(outgoing, ('dom', 'sub'), split_axis=0, concat_axis=0, til...  23.3 us
    pallas_call x1, Pallas kernels, gather_rows(): pl.pallas_call(gather_rows_kernel, grid=(peers // PEER_STEP,), in_specs=[...  19 us
    pallas_call x1, Pallas kernels, inner_aggregate(): pl.pallas_call(inner_kernel, grid_spec=pltpu.PrefetchScalarGridSpec(num_s...  12.9 us
    pallas_call x1, Pallas kernels, gather_scores(): pl.pallas_call(gather_scores_kernel, grid=(peers // PEER_STEP,), in_specs...  9.8 us
    pallas_call x1, Pallas kernels, outer_aggregate(): pl.pallas_call(outer_kernel, grid_spec=pltpu.PrefetchScalarGridSpec(num_s...  9.65 us
  transfers between devices with their start and end apart: 2, of which 2 were waited for; matrix products, arithmetic and copies ran while one was open for 1% of the time, Pallas kernels for 0%

profile of v1, /device:TPU:1, one launch (start us, length us, event | category | flops | bytes accessed | tf_op | source)
XLA Modules:
  0.0 206.5 jit_solution(418643782842908703)
XLA Ops:
  0.0 0.0 copy-start
  0.0 0.8 convert_rsqrt_fusion
  0.8 0.5 copy-done
  1.3 0.0 copy-start.2
  1.3 2.4 %fusion.rows_ref = bf16[1024,256]{1,0:T(8,128)(2,1)} fusion(bf16[1024,602]{0,1:T(8,128)(2,1)S(1)} %copy-done, bf16[602,256]{1,0:T(8,128)(2,1)} %param.10, f32[1024]{0:T(1024)S(1)} %convert_rsqrt_fusion), kind=kOutput, calls=%fused_computation.1 | convolution fusion | flops 316145664 | bytes 2069504 | tf_op jit(solution)/shard_map/dot_general | solution.py:189
  3.7 19.0 %gather_rows.1 = bf16[128,128,256]{2,1,0:T(8,128)(2,1)} custom-call(s32[128,128]{1,0:T(8,128)} %bitcast.22, bf16[1024,256]{1,0:T(8,128)(2,1)} %fusion.rows_ref), custom_call_target="tpu_custom_call" | custom-call | tf_op jit(solution)/shard_map/gather_rows/pallas_call | solution.py:27
  22.7 0.0 copy-start.3
  22.7 11.9 %all-to-all-start = ((bf16[128,128,256]{2,1,0:T(8,128)(2,1)}), bf16[128,128,256]{2,1,0:T(8,128)(2,1)}, u32[]{:S(2)}, u32[]{:S(2)}) async-start(bf16[128,128,256]{2,1,0:T(8,128)(2,1)} %gather_rows.1), calls=%async_computation | async-start | bytes 16777216 | tf_op jit(solution)/shard_map/all_to_all | solution.py:177
  34.6 0.0 copy-done.2
  34.7 1.0 copy.12.inv_ref
  35.7 0.0 copy-done.3
  35.7 0.6 pad.8.w_ref
  36.3 97.2 %all-to-all-done.arrived_ref = bf16[128,128,256]{2,1,0:T(8,128)(2,1)} async-done(((bf16[128,128,256]{2,1,0:T(8,128)(2,1)}), bf16[128,128,256]{2,1,0:T(8,128)(2,1)}, u32[]{:S(2)}, u32[]{:S(2)}) %all-to-all-start) | async-done | bytes 8388640 | tf_op jit(solution)/shard_map/all_to_all | solution.py:177
  133.5 12.9 %inner_aggregate.1.own_ref = bf16[48,1024]{1,0:T(8,128)(2,1)} custom-call(s32[8,32]{1,0:T(8,128)} %cols_ref.3, bf16[8,32,128,128]{3,2,1,0:T(8,128)(2,1)} %tiles_ref.3, bf16[8,128,256]{2,1,0:T(8,128)(2,1)} %bitcast.19, bf16[128,128,256]{2,1,0:T(8,128)(2,1)} %all-to-all-done.arrived_ref, f32[1024,1]{1,0:T(8,128)} %copy.12.inv_ref, f32[1,256]{1,0:T(1,128)} %bitcast.27, ...), custom_call_target="tpu_custom_call" | custom-call | tf_op jit(solution)/shard_map/inner_aggregate/pallas_call | solution.py:71
  146.5 1.5 copy.17
  148.0 9.8 %gather_scores.1 = bf16[128,48,128]{2,1,0:T(8,128)(2,1)} custom-call(s32[128,128]{1,0:T(8,128)} %bitcast.23, bf16[192,256]{1,0:T(8,128)(2,1)} %bitcast.21), custom_call_target="tpu_custom_call" | custom-call | tf_op jit(solution)/shard_map/gather_scores/pallas_call | solution.py:119
  157.8 0.0 copy-start.4
  157.8 11.4 %all-to-all-start.1 = ((bf16[128,48,128]{2,1,0:T(8,128)(2,1)}), bf16[128,48,128]{2,1,0:T(8,128)(2,1)S(1)}, u32[]{:S(2)}, u32[]{:S(2)}) async-start(bf16[128,48,128]{2,1,0:T(8,128)(2,1)} %gather_scores.1), calls=%async_computation.1 | async-start | bytes 3145728 | tf_op jit(solution)/shard_map/all_to_all | solution.py:177
  169.2 0.0 copy-done.4
  169.3 0.7 copy.14.bias_ref
  170.0 24.1 %all-to-all-done.1.arrived_ref = bf16[128,48,128]{2,1,0:T(8,128)(2,1)S(1)} async-done(((bf16[128,48,128]{2,1,0:T(8,128)(2,1)}), bf16[128,48,128]{2,1,0:T(8,128)(2,1)S(1)}, u32[]{:S(2)}, u32[]{:S(2)}) %all-to-all-start.1) | async-done | bytes 1572896 | tf_op jit(solution)/shard_map/all_to_all | solution.py:177
  194.0 0.0 copy-start.1
  194.0 1.1 copy-done.1
  195.2 9.7 %outer_aggregate.1 = f32[48,1024]{1,0:T(8,128)} custom-call(s32[8,32]{1,0:T(8,128)} %cols_ref.3, bf16[8,32,128,128]{3,2,1,0:T(8,128)(2,1)} %tiles_ref.3, bf16[48,1024]{1,0:T(8,128)(2,1)} %inner_aggregate.1.own_ref, bf16[128,48,128]{2,1,0:T(8,128)(2,1)} %copy-done.1, f32[1,1024]{1,0:T(1,128)} %bitcast.25, f32[48,1]{1,0:T(8,128)} %copy.14.bias_ref), custom_call_target="tpu_custom_call" | custom-call | tf_op jit(solution)/shard_map/outer_aggregate/pallas_call | solution.py:156
  204.8 1.6 slice_bitcast_fusion
  (1 shorter events, 0.0 us)
Async XLA Ops:
  0.0 1.3 copy-start
  1.3 33.3 %copy-start.2 = (f32[1024]{0:T(1024)}, f32[1024]{0:T(1024)S(1)}, u32[]{:S(2)}) copy-start(f32[1024]{0:T(1024)S(1)} %convert_rsqrt_fusion) | copy-start | bytes 12292
  22.7 13.0 %copy-start.3 = (bf16[256,41]{0,1:T(8,128)(2,1)S(1)}, bf16[256,41]{0,1:T(8,128)(2,1)}, u32[]{:S(2)}) copy-start(bf16[256,41]{0,1:T(8,128)(2,1)} %param.12) | copy-start | bytes 62980
  22.7 110.8 %all-to-all-start = ((bf16[128,128,256]{2,1,0:T(8,128)(2,1)}), bf16[128,128,256]{2,1,0:T(8,128)(2,1)}, u32[]{:S(2)}, u32[]{:S(2)}) async-start(bf16[128,128,256]{2,1,0:T(8,128)(2,1)} %gather_rows.1), calls=%async_computation | async-start | bytes 16777216 | tf_op jit(solution)/shard_map/all_to_all | solution.py:177
  157.8 11.4 %copy-start.4 = (f32[41]{0:T(128)S(1)}, f32[41]{0:T(128)}, u32[]{:S(2)}) copy-start(f32[41]{0:T(128)} %param.13) | copy-start | bytes 496
  157.8 36.2 %all-to-all-start.1 = ((bf16[128,48,128]{2,1,0:T(8,128)(2,1)}), bf16[128,48,128]{2,1,0:T(8,128)(2,1)S(1)}, u32[]{:S(2)}, u32[]{:S(2)}) async-start(bf16[128,48,128]{2,1,0:T(8,128)(2,1)} %gather_scores.1), calls=%async_computation.1 | async-start | bytes 3145728 | tf_op jit(solution)/shard_map/all_to_all | solution.py:177
  194.0 1.1 copy-start.1

commit v2 on v0

v2 whole, which is shorter than its diff:
```python
import jax
import jax.numpy as jnp
from jax import lax
from jax.experimental import pallas as pl
from jax.experimental.pallas import tpu as pltpu
from jax.sharding import PartitionSpec as P

BLOCK = 128
ROW_LISTS = 16
SCORE_LISTS = 32
QUARTER = 256
TILE_GROUPS = 4
NT = (((1,), (1,)), ((), ()))
MIB = 2**20


def whole():
    return pl.BlockSpec(memory_space=pltpu.VMEM)


def in_hbm(array):
    return pltpu.with_memory_space_constraint(array, pltpu.HBM)


def anywhere():
    return pl.BlockSpec(memory_space=pltpu.HBM)


def front_kernel(lists_ref, features_ref, w_ref, degrees_ref, sent_ref, own_ref, pick_ref):
    height = own_ref.shape[0]

    @pl.when(pl.program_id(0) == 0)
    def _():
        inv = lax.rsqrt(degrees_ref[...].astype(jnp.float32)).T
        for r in range(height // BLOCK):
            part = lax.dot_general(
                features_ref[:, r * BLOCK : (r + 1) * BLOCK],
                w_ref[...],
                (((0,), (0,)), ((), ())),
                preferred_element_type=jnp.float32,
            )
            own_ref[r * BLOCK : (r + 1) * BLOCK] = (part * inv[:, r : r + 1]).astype(jnp.bfloat16)

    by_slot = lists_ref[...].T
    row_of_lane = lax.broadcasted_iota(jnp.int32, (BLOCK, height), 1)
    for p in range(ROW_LISTS):
        pick_ref[p * BLOCK : (p + 1) * BLOCK] = (
            (by_slot[:, p : p + 1] == row_of_lane).astype(jnp.float32).astype(jnp.bfloat16)
        )
    rows = jnp.dot(pick_ref[...], own_ref[...], preferred_element_type=jnp.float32)
    sent_ref[...] = rows.astype(jnp.bfloat16).reshape(sent_ref.shape)


def front(lists, features_t, w_inner, degrees):
    peers = lists.shape[0]
    height = features_t.shape[1]
    width = w_inner.shape[1]
    return pl.pallas_call(
        front_kernel,
        grid=(peers // ROW_LISTS,),
        in_specs=[
            pl.BlockSpec((ROW_LISTS, BLOCK), lambda g: (g, 0)),
            pl.BlockSpec(features_t.shape, lambda g: (0, 0)),
            pl.BlockSpec(w_inner.shape, lambda g: (0, 0)),
            pl.BlockSpec(degrees.shape, lambda g: (0, 0)),
        ],
        out_specs=[
            pl.BlockSpec((ROW_LISTS, BLOCK, width), lambda g: (g, 0, 0)),
            pl.BlockSpec((height, width), lambda g: (0, 0)),
        ],
        out_shape=[
            jax.ShapeDtypeStruct((peers, BLOCK, width), jnp.bfloat16),
            jax.ShapeDtypeStruct((height, width), jnp.bfloat16),
        ],
        scratch_shapes=[pltpu.VMEM((ROW_LISTS * BLOCK, height), jnp.bfloat16)],
        name="front",
    )(lists, features_t, w_inner, degrees)


def fetch_tiles(tiles_ref, near_ref, sems):
    size = tiles_ref.shape[0] // TILE_GROUPS
    return [
        pltpu.make_async_copy(
            tiles_ref.at[pl.ds(g * size, size)], near_ref.at[pl.ds(g * size, size)], sems.at[g]
        )
        for g in range(TILE_GROUPS)
    ]


def inner_kernel(
    cols_ref, tiles_ref, own_ref, arrived_ref, degrees_ref, bias_ref, w_ref, out_ref, space, near, space_sems, tile_sems
):
    row_blocks, count = tiles_ref.shape[:2]
    own_blocks, peers = own_ref.shape[0], arrived_ref.shape[0]
    classes = out_ref.shape[0] // (row_blocks * BLOCK // QUARTER)
    copies = [
        pltpu.make_async_copy(arrived_ref, space.at[pl.ds(own_blocks, peers)], space_sems.at[0]),
        pltpu.make_async_copy(own_ref, space.at[pl.ds(0, own_blocks)], space_sems.at[1]),
    ]
    tile_copies = fetch_tiles(tiles_ref, near, tile_sems)
    for copy in copies:
        copy.start()
    tile_copies[0].start()
    inv = lax.rsqrt(degrees_ref[...].astype(jnp.float32)).T
    for copy in copies:
        copy.wait()
    for copy in tile_copies[1:]:
        copy.start()
    for r in range(row_blocks):
        if r % (row_blocks // TILE_GROUPS) == 0:
            tile_copies[r // (row_blocks // TILE_GROUPS)].wait()
        left = jnp.concatenate([near[r, t] for t in range(count)], axis=1)
        right = jnp.concatenate([space[cols_ref[r, t]] for t in range(count)], axis=0)
        total = jnp.dot(left, right, preferred_element_type=jnp.float32)
        scale = inv[:, r : r + 1]
        hidden = (scale * jnp.maximum(scale * total + bias_ref[...], 0.0)).astype(jnp.bfloat16)
        scores = lax.dot_general(w_ref[...], hidden, NT, preferred_element_type=jnp.float32)
        quarter, side = divmod(r * BLOCK, QUARTER)
        out_ref[quarter * classes : (quarter + 1) * classes, side : side + BLOCK] = scores.astype(jnp.bfloat16)


def inner_aggregate(tile_col, tiles, own, arrived, degrees, bias, w_t):
    row_blocks = tiles.shape[0]
    return pl.pallas_call(
        inner_kernel,
        in_specs=[pl.BlockSpec(memory_space=pltpu.SMEM)] + [anywhere()] * 3 + [whole()] * 3,
        out_specs=whole(),
        out_shape=jax.ShapeDtypeStruct((w_t.shape[0] * row_blocks * BLOCK // QUARTER, QUARTER), jnp.bfloat16),
        scratch_shapes=[
            pltpu.VMEM((own.shape[0] + arrived.shape[0],) + own.shape[1:], jnp.bfloat16),
            pltpu.VMEM(tiles.shape, jnp.bfloat16),
            pltpu.SemaphoreType.DMA((2,)),
            pltpu.SemaphoreType.DMA((TILE_GROUPS,)),
        ],
        compiler_params=pltpu.CompilerParams(vmem_limit_bytes=32 * MIB),
        name="inner_aggregate",
    )(tile_col, in_hbm(tiles), own, arrived, degrees, bias, w_t)


def gather_scores_kernel(lists_ref, stacked_ref, out_ref):
    classes = out_ref.shape[1]
    stacked = stacked_ref[...]
    group = 8
    row_of_sublane = lax.broadcasted_iota(jnp.int32, (QUARTER, group * BLOCK), 0)
    for p in range(0, SCORE_LISTS, group):
        index = jnp.concatenate([lists_ref[p + k : p + k + 1] for k in range(group)], axis=1)
        low = jnp.bitwise_and(index, QUARTER - 1)
        quarter = jnp.right_shift(index, QUARTER.bit_length() - 1)
        pick = (low == row_of_sublane).astype(jnp.float32).astype(jnp.bfloat16)
        every = jnp.dot(stacked, pick, preferred_element_type=jnp.float32)
        chosen = jnp.zeros((classes, group * BLOCK), jnp.float32)
        for q in range(stacked_ref.shape[0] // classes):
            chosen = jnp.where(quarter == q, every[q * classes : (q + 1) * classes], chosen)
        chosen = chosen.astype(jnp.bfloat16)
        for k in range(group):
            out_ref[p + k] = chosen[:, k * BLOCK : (k + 1) * BLOCK]


def gather_scores(lists, stacked, classes):
    peers = lists.shape[0]
    return pl.pallas_call(
        gather_scores_kernel,
        grid=(peers // SCORE_LISTS,),
        in_specs=[
            pl.BlockSpec((SCORE_LISTS, BLOCK), lambda g: (g, 0)),
            pl.BlockSpec(stacked.shape, lambda g: (0, 0)),
        ],
        out_specs=pl.BlockSpec((SCORE_LISTS, classes, BLOCK), lambda g: (g, 0, 0)),
        out_shape=pltpu.HBM((peers, classes, BLOCK), jnp.bfloat16),
        compiler_params=pltpu.CompilerParams(vmem_limit_bytes=16 * MIB),
        name="gather_scores",
    )(lists, stacked)


def outer_kernel(cols_ref, tiles_ref, stacked_ref, arrived_ref, degrees_ref, bias_ref, out_ref, space, near, tile_sems):
    row_blocks, count = tiles_ref.shape[:2]
    padded = arrived_ref.shape[1]
    classes = out_ref.shape[0]
    tile_copies = fetch_tiles(tiles_ref, near, tile_sems)
    for copy in tile_copies:
        copy.start()
    for r in range(row_blocks):
        quarter, side = divmod(r * BLOCK, QUARTER)
        space[r] = stacked_ref[quarter * padded : (quarter + 1) * padded, side : side + BLOCK]
    space[row_blocks:] = arrived_ref[...]
    inv = lax.rsqrt(degrees_ref[...].astype(jnp.float32))
    bias = bias_ref[...].T
    for r in range(row_blocks):
        if r % (row_blocks // TILE_GROUPS) == 0:
            tile_copies[r // (row_blocks // TILE_GROUPS)].wait()
        left = jnp.concatenate([near[r, t] for t in range(count)], axis=1)
        right = jnp.concatenate([space[cols_ref[r, t]] for t in range(count)], axis=1)
        total = lax.dot_general(left, right, NT, preferred_element_type=jnp.float32).T
        out_ref[:, r * BLOCK : (r + 1) * BLOCK] = inv[r : r + 1] * total[:classes] + bias


def outer_aggregate(tile_col, tiles, stacked, arrived, degrees, bias):
    row_blocks = tiles.shape[0]
    peers, padded, _ = arrived.shape
    return pl.pallas_call(
        outer_kernel,
        in_specs=[pl.BlockSpec(memory_space=pltpu.SMEM), anywhere()] + [whole()] * 4,
        out_specs=whole(),
        out_shape=jax.ShapeDtypeStruct((bias.shape[1], row_blocks * BLOCK), jnp.float32),
        scratch_shapes=[
            pltpu.VMEM((row_blocks + peers, padded, BLOCK), jnp.bfloat16),
            pltpu.VMEM(tiles.shape, jnp.bfloat16),
            pltpu.SemaphoreType.DMA((TILE_GROUPS,)),
        ],
        compiler_params=pltpu.CompilerParams(vmem_limit_bytes=24 * MIB),
        name="outer_aggregate",
    )(tile_col, in_hbm(tiles), stacked, arrived, degrees, bias)


def exchange(outgoing):
    return lax.all_to_all(outgoing, ("dom", "sub"), split_axis=0, concat_axis=0, tiled=True)


def on_device(
    features, w_inner, bias_inner, w_outer, bias_outer, tiles, tile_col, degrees, send_rows
):
    lists = send_rows[0]
    classes = w_outer.shape[1]
    padded = 16 * ((classes + 15) // 16)
    width = w_inner.shape[1]
    degree_rows = degrees.reshape(-1, BLOCK)
    outgoing, own = front(lists, features.T, w_inner, degree_rows)
    arrived = exchange(outgoing)
    w_t = jnp.pad(w_outer.T, ((0, padded - classes), (0, 0)))
    stacked = inner_aggregate(
        tile_col, tiles, own.reshape(-1, BLOCK, width), arrived, degree_rows, bias_inner[None, :], w_t
    )
    arrived_scores = exchange(gather_scores(lists, stacked, padded))
    logits_t = outer_aggregate(
        tile_col, tiles, stacked, arrived_scores, degree_rows, bias_outer[None, :]
    )
    return logits_t.T


def solution(mesh):
    return jax.shard_map(
        on_device,
        mesh=mesh,
        in_specs=(
            P(("dom", "sub"), None),
            P(),
            P(),
            P(),
            P(),
            P(("dom", "sub"), None, None, None),
            P(("dom", "sub"), None),
            P(("dom", "sub")),
            P(("dom", "sub"), None, None),
        ),
        out_specs=P(("dom", "sub"), None),
        check_vma=False,
    )
```

time: 437 us -> 182 us (0.42)
  local copies, waits for them, and re-layouts: 181 us -> 0.04 us
  waiting for transfers between devices: 152 us -> 98.9 us
  other arithmetic: 44.1 us -> 0 us
  blocking collectives: 0 us -> 36.2 us
  Pallas kernels: 0 us -> 35.1 us
  matrix products: 33.7 us -> 0 us
  starting transfers between devices: 23.8 us -> 11.9 us
    gather x18 -> x0, local copies, waits for them, and re-layouts: 181 us -> none  [the longest x2 123 us: aggregate(): jnp.take(feature_rows, clipped, axis=0)]
    all_to_all x2 -> x1, waiting for transfers between devices: 152 us -> 98.9 us  [exchange(): lax.all_to_all(outgoing, ('dom', 'sub'), split_axis=0, concat_axis=0, til...]
    all_to_all x0 -> x1, blocking collectives: none -> 36.2 us  [exchange(): lax.all_to_all(outgoing, ('dom', 'sub'), split_axis=0, concat_axis=0, til...]
    pallas_call x0 -> x4, Pallas kernels: none -> 35.1 us  [the longest x1 14.3 us: front(): pl.pallas_call(front_kernel, grid=(peers // ROW_LISTS,), in_specs=[pl.Blo...]
    dot_general x18 -> x0, matrix products: 33.7 us -> none  [the longest x16 31.8 us: rowblock(): jnp.einsum('tij,tjw->iw', tile_set, blocks, preferred_element_type=jnp.fl...]
    select_n x18 -> x0, other arithmetic: 26.2 us -> none  [the longest x2 15.1 us: aggregate(): jnp.where(live_slot, jnp.take(feature_rows, clipped, axis=0), jnp.zeros((...]
    concatenate x2 -> x0, other arithmetic: 12.2 us -> none  [aggregate(): jnp.concatenate([feature_rows.reshape(-1, block_rows, width), arrived], a...]
    all_to_all x2 -> x1, starting transfers between devices: 23.8 us -> 11.9 us  [exchange(): lax.all_to_all(outgoing, ('dom', 'sub'), split_axis=0, concat_axis=0, til...]
  transfers between devices with their start and end apart: 2 -> 1, of which waited for: 2 -> 1; matrix products, arithmetic and copies ran while one was open for 0% -> 0% of each run, Pallas kernels for 0% -> 0%
where the time goes in v2:
time: 182 us
  waiting for transfers between devices  98.9 us (54%)
  blocking collectives  36.2 us (20%)
  Pallas kernels  35.1 us (19%)
  starting transfers between devices  11.9 us (7%)
    all_to_all x1, waiting for transfers between devices, exchange(): lax.all_to_all(outgoing, ('dom', 'sub'), split_axis=0, concat_axis=0, til...  98.9 us
    all_to_all x1, blocking collectives, exchange(): lax.all_to_all(outgoing, ('dom', 'sub'), split_axis=0, concat_axis=0, til...  36.2 us
    pallas_call x1, Pallas kernels, front(): pl.pallas_call(front_kernel, grid=(peers // ROW_LISTS,), in_specs=[pl.Blo...  14.3 us
    all_to_all x1, starting transfers between devices, exchange(): lax.all_to_all(outgoing, ('dom', 'sub'), split_axis=0, concat_axis=0, til...  11.9 us
    pallas_call x1, Pallas kernels, inner_aggregate(): pl.pallas_call(inner_kernel, in_specs=[pl.BlockSpec(memory_space=pltpu.SM...  10.7 us
    pallas_call x1, Pallas kernels, outer_aggregate(): pl.pallas_call(outer_kernel, in_specs=[pl.BlockSpec(memory_space=pltpu.SM...  5.85 us
    pallas_call x1, Pallas kernels, gather_scores(): pl.pallas_call(gather_scores_kernel, grid=(peers // SCORE_LISTS,), in_spe...  4.23 us
  transfers between devices with their start and end apart: 1, of which 1 were waited for; matrix products, arithmetic and copies ran while one was open for 0% of the time, Pallas kernels for 0%

profile of v2, /device:TPU:1, one launch (start us, length us, event | category | flops | bytes accessed | tf_op | source)
XLA Modules:
  0.0 182.2 jit_solution(12294819481329137565)
XLA Ops:
  0.0 14.3 %front.1 = (bf16[128,128,256]{2,1,0:T(8,128)(2,1)}, bf16[1024,256]{1,0:T(8,128)(2,1)}) custom-call(s32[128,128]{1,0:T(8,128)} %bitcast.9, bf16[602,1024]{1,0:T(8,128)(2,1)} %bitcast.16, bf16[602,256]{1,0:T(8,128)(2,1)} %w_ref.1, s32[8,128]{1,0:T(8,128)} %bitcast.11), custom_call_target="tpu_custom_call" | custom-call | tf_op jit(solution)/shard_map/front/pallas_call | solution.py:58
  14.3 0.0 copy-start.6
  14.3 0.0 copy-start
  14.3 0.0 copy-start.2
  14.3 0.0 copy-start.3
  14.3 0.0 copy-start.4
  14.3 11.9 %all-to-all-start = ((bf16[128,128,256]{2,1,0:T(8,128)(2,1)}), bf16[128,128,256]{2,1,0:T(8,128)(2,1)}, u32[]{:S(2)}, u32[]{:S(2)}) async-start(bf16[128,128,256]{2,1,0:T(8,128)(2,1)} %get-tuple-element.8), calls=%async_computation | async-start | bytes 16777216 | tf_op jit(solution)/shard_map/all_to_all | solution.py:216
  26.3 0.0 copy-done.6
  26.3 98.9 %all-to-all-done.arrived_ref = bf16[128,128,256]{2,1,0:T(8,128)(2,1)} async-done(((bf16[128,128,256]{2,1,0:T(8,128)(2,1)}), bf16[128,128,256]{2,1,0:T(8,128)(2,1)}, u32[]{:S(2)}, u32[]{:S(2)}) %all-to-all-start) | async-done | bytes 8388640 | tf_op jit(solution)/shard_map/all_to_all | solution.py:216
  125.2 0.0 copy-done
  125.2 0.0 copy-done.2
  125.2 0.0 copy-done.3
  125.2 0.0 copy-done.4
  125.2 0.0 copy-start.1
  125.2 0.0 copy-start.5
  125.2 10.7 %inner_aggregate.1.stacked_ref = bf16[192,256]{1,0:T(8,128)(2,1)S(1)} custom-call(s32[8,32]{1,0:T(8,128)S(1)} %copy-done.3, bf16[8,32,128,128]{3,2,1,0:T(8,128)(2,1)} %tiles_ref.3, bf16[8,128,256]{2,1,0:T(8,128)(2,1)S(1)} %bitcast.8, bf16[128,128,256]{2,1,0:T(8,128)(2,1)} %all-to-all-done.arrived_ref, s32[8,128]{1,0:T(8,128)S(1)} %bitcast.12, ...), custom_call_target="tpu_custom_call" | custom-call | tf_op jit(solution)/shard_map/inner_aggregate/pallas_call | solution.py:124
  135.9 0.0 copy-done.1
  135.9 4.2 %gather_scores.1 = bf16[128,48,128]{2,1,0:T(8,128)(2,1)} custom-call(s32[128,128]{1,0:T(8,128)S(1)} %bitcast.10, bf16[192,256]{1,0:T(8,128)(2,1)S(1)} %inner_aggregate.1.stacked_ref), custom_call_target="tpu_custom_call" | custom-call | tf_op jit(solution)/shard_map/gather_scores/pallas_call | solution.py:161
  140.2 36.2 %all_to_all.10.arrived_ref = bf16[128,48,128]{2,1,0:T(8,128)(2,1)S(1)} all-to-all(bf16[128,48,128]{2,1,0:T(8,128)(2,1)} %gather_scores.1), channel_id=1, replica_groups=mesh['dom'=16,'sub'=8] {'dom','sub'}, dimensions={0} | all-to-all | bytes 3145728 | tf_op jit(solution)/shard_map/all_to_all | solution.py:216
  176.4 0.0 copy-done.5
  176.4 5.9 %outer_aggregate.1 = f32[41,1024]{1,0:T(8,128)} custom-call(s32[8,32]{1,0:T(8,128)S(1)} %copy-done.3, bf16[8,32,128,128]{3,2,1,0:T(8,128)(2,1)} %tiles_ref.3, bf16[192,256]{1,0:T(8,128)(2,1)S(1)} %inner_aggregate.1.stacked_ref, bf16[128,48,128]{2,1,0:T(8,128)(2,1)S(1)} %all_to_all.10.arrived_ref, s32[8,128]{1,0:T(8,128)S(1)} %bitcast.13, f32[1,41]{1,0:T(1,128)S(1)} %bitcast.15), custom_call_target="tpu_custom_call" | custom-call | tf_op jit(solution)/shard_map/outer_aggregate/pallas_call | solution.py:200
  (1 shorter events, 0.0 us)
Async XLA Ops:
  14.3 12.0 %copy-start.6 = (bf16[256,41]{0,1:T(8,128)(2,1)S(1)}, bf16[256,41]{0,1:T(8,128)(2,1)}, u32[]{:S(2)}) copy-start(bf16[256,41]{0,1:T(8,128)(2,1)} %param.12) | copy-start | bytes 62980
  14.3 110.9 %copy-start = (bf16[1024,256]{1,0:T(8,128)(2,1)S(1)}, bf16[1024,256]{1,0:T(8,128)(2,1)}, u32[]{:S(2)}) copy-start(bf16[1024,256]{1,0:T(8,128)(2,1)} %get-tuple-element.7) | copy-start | bytes 1572868
  14.3 110.9 %copy-start.2 = (s32[1024]{0:T(1024)S(1)}, s32[1024]{0:T(1024)}, u32[]{:S(2)}) copy-start(s32[1024]{0:T(1024)} %param.16) | copy-start | bytes 12292
  14.3 110.9 %copy-start.3 = (s32[8,32]{1,0:T(8,128)S(1)}, s32[8,32]{1,0:T(8,128)}, u32[]{:S(2)}) copy-start(s32[8,32]{1,0:T(8,128)} %cols_ref.3) | copy-start | bytes 3076
  14.3 110.9 %copy-start.4 = (f32[256]{0:T(256)S(1)}, f32[256]{0:T(256)}, u32[]{:S(2)}) copy-start(f32[256]{0:T(256)} %param.11) | copy-start | bytes 3076
  14.3 110.8 %all-to-all-start = ((bf16[128,128,256]{2,1,0:T(8,128)(2,1)}), bf16[128,128,256]{2,1,0:T(8,128)(2,1)}, u32[]{:S(2)}, u32[]{:S(2)}) async-start(bf16[128,128,256]{2,1,0:T(8,128)(2,1)} %get-tuple-element.8), calls=%async_computation | async-start | bytes 16777216 | tf_op jit(solution)/shard_map/all_to_all | solution.py:216
  125.2 10.8 %copy-start.1 = (s32[1,128,128]{2,1,0:T(8,128)S(1)}, s32[1,128,128]{2,1,0:T(8,128)}, u32[]{:S(2)}) copy-start(s32[1,128,128]{2,1,0:T(8,128)} %param.17) | copy-start | bytes 196612
  125.2 51.2 %copy-start.5 = (f32[41]{0:T(128)S(1)}, f32[41]{0:T(128)}, u32[]{:S(2)}) copy-start(f32[41]{0:T(128)} %param.13) | copy-start | bytes 496

commit v3 on v2

--- a/solution.py
+++ b/solution.py
@@ -6,10 +6,11 @@
 from jax.sharding import PartitionSpec as P
 
 BLOCK = 128
-ROW_LISTS = 16
-SCORE_LISTS = 32
+ROW_LISTS = 32
+SCORE_LISTS = 8
 QUARTER = 256
 TILE_GROUPS = 4
+SENDS = 4
 NT = (((1,), (1,)), ((), ()))
 MIB = 2**20
 
@@ -88,11 +89,31 @@
 
 
 def inner_kernel(
-    cols_ref, tiles_ref, own_ref, arrived_ref, degrees_ref, bias_ref, w_ref, out_ref, space, near, space_sems, tile_sems
+    cols_ref,
+    lists_ref,
+    tiles_ref,
+    own_ref,
+    arrived_ref,
+    degrees_ref,
+    bias_ref,
+    w_ref,
+    stacked_ref,
+    sent_ref,
+    space,
+    near,
+    picks,
+    hidden,
+    outgoing,
+    space_sems,
+    tile_sems,
+    sent_sems,
 ):
     row_blocks, count = tiles_ref.shape[:2]
     own_blocks, peers = own_ref.shape[0], arrived_ref.shape[0]
-    classes = out_ref.shape[0] // (row_blocks * BLOCK // QUARTER)
+    padded = outgoing.shape[1]
+    classes = w_ref.shape[0]
+    quarters = stacked_ref.shape[0] // padded
+    steps = peers // SCORE_LISTS
     copies = [
         pltpu.make_async_copy(arrived_ref, space.at[pl.ds(own_blocks, peers)], space_sems.at[0]),
         pltpu.make_async_copy(own_ref, space.at[pl.ds(0, own_blocks)], space_sems.at[1]),
@@ -101,6 +122,16 @@
     for copy in copies:
         copy.start()
     tile_copies[0].start()
+
+    def list_row(g):
+        rows = lists_ref[g * SCORE_LISTS : (g + 1) * SCORE_LISTS]
+        return jnp.concatenate([rows[k : k + 1] for k in range(SCORE_LISTS)], axis=1)
+
+    row_of_sublane = lax.broadcasted_iota(jnp.int32, (QUARTER, SCORE_LISTS * BLOCK), 0)
+    for g in range(steps):
+        low = jnp.bitwise_and(list_row(g), QUARTER - 1)
+        picks[g] = (low == row_of_sublane).astype(jnp.float32).astype(jnp.bfloat16)
+
     inv = lax.rsqrt(degrees_ref[...].astype(jnp.float32)).T
     for copy in copies:
         copy.wait()
@@ -113,63 +144,61 @@
         right = jnp.concatenate([space[cols_ref[r, t]] for t in range(count)], axis=0)
         total = jnp.dot(left, right, preferred_element_type=jnp.float32)
         scale = inv[:, r : r + 1]
-        hidden = (scale * jnp.maximum(scale * total + bias_ref[...], 0.0)).astype(jnp.bfloat16)
-        scores = lax.dot_general(w_ref[...], hidden, NT, preferred_element_type=jnp.float32)
-        quarter, side = divmod(r * BLOCK, QUARTER)
-        out_ref[quarter * classes : (quarter + 1) * classes, side : side + BLOCK] = scores.astype(jnp.bfloat16)
-
-
-def inner_aggregate(tile_col, tiles, own, arrived, degrees, bias, w_t):
+        row = scale * jnp.maximum(scale * total + bias_ref[...], 0.0)
+        hidden[r * BLOCK : (r + 1) * BLOCK] = row.astype(jnp.bfloat16)
+
+    scores = lax.dot_general(w_ref[...], hidden[...], NT, preferred_element_type=jnp.float32)
+    scores = jnp.concatenate([scores, jnp.zeros((padded - classes, scores.shape[1]), jnp.float32)], axis=0)
+    scores = scores.astype(jnp.bfloat16)
+    for q in range(quarters):
+        stacked_ref[q * padded : (q + 1) * padded] = scores[:, q * QUARTER : (q + 1) * QUARTER]
+
+    sends = []
+    per_send = steps // SENDS
+    for g in range(steps):
+        quarter = jnp.right_shift(list_row(g), QUARTER.bit_length() - 1)
+        every = jnp.dot(stacked_ref[...], picks[g], preferred_element_type=jnp.float32)
+        chosen = jnp.zeros((padded, SCORE_LISTS * BLOCK), jnp.float32)
+        for q in range(quarters):
+            chosen = jnp.where(quarter == q, every[q * padded : (q + 1) * padded], chosen)
+        chosen = chosen.astype(jnp.bfloat16)
+        for k in range(SCORE_LISTS):
+            outgoing[g * SCORE_LISTS + k] = chosen[:, k * BLOCK : (k + 1) * BLOCK]
+        if (g + 1) % per_send == 0:
+            first = (g + 1 - per_send) * SCORE_LISTS
+            part = pl.ds(first, per_send * SCORE_LISTS)
+            send = pltpu.make_async_copy(outgoing.at[part], sent_ref.at[part], sent_sems.at[g // per_send])
+            send.start()
+            sends.append(send)
+    for send in sends:
+        send.wait()
+
+
+def inner_aggregate(tile_col, lists, tiles, own, arrived, degrees, bias, w_t, padded):
     row_blocks = tiles.shape[0]
+    peers, _, width = arrived.shape
+    height = row_blocks * BLOCK
     return pl.pallas_call(
         inner_kernel,
-        in_specs=[pl.BlockSpec(memory_space=pltpu.SMEM)] + [anywhere()] * 3 + [whole()] * 3,
-        out_specs=whole(),
-        out_shape=jax.ShapeDtypeStruct((w_t.shape[0] * row_blocks * BLOCK // QUARTER, QUARTER), jnp.bfloat16),
+        in_specs=[pl.BlockSpec(memory_space=pltpu.SMEM), whole()] + [anywhere()] * 3 + [whole()] * 3,
+        out_specs=[whole(), anywhere()],
+        out_shape=[
+            jax.ShapeDtypeStruct((padded * height // QUARTER, QUARTER), jnp.bfloat16),
+            pltpu.HBM((peers, padded, BLOCK), jnp.bfloat16),
+        ],
         scratch_shapes=[
-            pltpu.VMEM((own.shape[0] + arrived.shape[0],) + own.shape[1:], jnp.bfloat16),
+            pltpu.VMEM((own.shape[0] + peers, BLOCK, width), jnp.bfloat16),
             pltpu.VMEM(tiles.shape, jnp.bfloat16),
+            pltpu.VMEM((peers // SCORE_LISTS, QUARTER, SCORE_LISTS * BLOCK), jnp.bfloat16),
+            pltpu.VMEM((height, width), jnp.bfloat16),
+            pltpu.VMEM((peers, padded, BLOCK), jnp.bfloat16),
             pltpu.SemaphoreType.DMA((2,)),
             pltpu.SemaphoreType.DMA((TILE_GROUPS,)),
-        ],
-        compiler_params=pltpu.CompilerParams(vmem_limit_bytes=32 * MIB),
+            pltpu.SemaphoreType.DMA((SENDS,)),
+        ],
+        compiler_params=pltpu.CompilerParams(vmem_limit_bytes=44 * MIB),
         name="inner_aggregate",
-    )(tile_col, in_hbm(tiles), own, arrived, degrees, bias, w_t)
-
-
-def gather_scores_kernel(lists_ref, stacked_ref, out_ref):
-    classes = out_ref.shape[1]
-    stacked = stacked_ref[...]
-    group = 8
-    row_of_sublane = lax.broadcasted_iota(jnp.int32, (QUARTER, group * BLOCK), 0)
-    for p in range(0, SCORE_LISTS, group):
-        index = jnp.concatenate([lists_ref[p + k : p + k + 1] for k in range(group)], axis=1)
-        low = jnp.bitwise_and(index, QUARTER - 1)
-        quarter = jnp.right_shift(index, QUARTER.bit_length() - 1)
-        pick = (low == row_of_sublane).astype(jnp.float32).astype(jnp.bfloat16)
-        every = jnp.dot(stacked, pick, preferred_element_type=jnp.float32)
-        chosen = jnp.zeros((classes, group * BLOCK), jnp.float32)
-        for q in range(stacked_ref.shape[0] // classes):
-            chosen = jnp.where(quarter == q, every[q * classes : (q + 1) * classes], chosen)
-        chosen = chosen.astype(jnp.bfloat16)
-        for k in range(group):
-            out_ref[p + k] = chosen[:, k * BLOCK : (k + 1) * BLOCK]
-
-
-def gather_scores(lists, stacked, classes):
-    peers = lists.shape[0]
-    return pl.pallas_call(
-        gather_scores_kernel,
-        grid=(peers // SCORE_LISTS,),
-        in_specs=[
-            pl.BlockSpec((SCORE_LISTS, BLOCK), lambda g: (g, 0)),
-            pl.BlockSpec(stacked.shape, lambda g: (0, 0)),
-        ],
-        out_specs=pl.BlockSpec((SCORE_LISTS, classes, BLOCK), lambda g: (g, 0, 0)),
-        out_shape=pltpu.HBM((peers, classes, BLOCK), jnp.bfloat16),
-        compiler_params=pltpu.CompilerParams(vmem_limit_bytes=16 * MIB),
-        name="gather_scores",
-    )(lists, stacked)
+    )(tile_col, lists, in_hbm(tiles), own, in_hbm(arrived), degrees, bias, w_t)
 
 
 def outer_kernel(cols_ref, tiles_ref, stacked_ref, arrived_ref, degrees_ref, bias_ref, out_ref, space, near, tile_sems):
@@ -226,11 +255,18 @@
     degree_rows = degrees.reshape(-1, BLOCK)
     outgoing, own = front(lists, features.T, w_inner, degree_rows)
     arrived = exchange(outgoing)
-    w_t = jnp.pad(w_outer.T, ((0, padded - classes), (0, 0)))
-    stacked = inner_aggregate(
-        tile_col, tiles, own.reshape(-1, BLOCK, width), arrived, degree_rows, bias_inner[None, :], w_t
+    stacked, outgoing_scores = inner_aggregate(
+        tile_col,
+        lists,
+        tiles,
+        own.reshape(-1, BLOCK, width),
+        arrived,
+        degree_rows,
+        bias_inner[None, :],
+        w_outer.T,
+        padded,
     )
-    arrived_scores = exchange(gather_scores(lists, stacked, padded))
+    arrived_scores = exchange(outgoing_scores)
     logits_t = outer_aggregate(
         tile_col, tiles, stacked, arrived_scores, degree_rows, bias_outer[None, :]
     )

time: 182 us -> 173 us (0.951)
  blocking collectives: 36.2 us -> 142 us
  waiting for transfers between devices: 98.9 us -> 0 us
  starting transfers between devices: 11.9 us -> 0 us
  Pallas kernels: 35.1 us -> 30.3 us
    all_to_all x1 -> x2, blocking collectives: 36.2 us -> 142 us  [exchange(): lax.all_to_all(outgoing, ('dom', 'sub'), split_axis=0, concat_axis=0, til...]
    all_to_all x1 -> x0, waiting for transfers between devices: 98.9 us -> none  [exchange(): lax.all_to_all(outgoing, ('dom', 'sub'), split_axis=0, concat_axis=0, til...]
    all_to_all x1 -> x0, starting transfers between devices: 11.9 us -> none  [exchange(): lax.all_to_all(outgoing, ('dom', 'sub'), split_axis=0, concat_axis=0, til...]
    pallas_call x1 -> x0, Pallas kernels: 4.23 us -> none  [gather_scores(): pl.pallas_call(gather_scores_kernel, grid=(peers // SCORE_LISTS,), in_spe...]
  transfers between devices with their start and end apart: 1 -> 0, of which waited for: 1 -> 0; matrix products, arithmetic and copies ran while one was open for 0% -> 0% of each run, Pallas kernels for 0% -> 0%
where the time goes in v3:
time: 173 us
  blocking collectives  142 us (82%)
  Pallas kernels  30.3 us (18%)
    all_to_all x2, blocking collectives, exchange(): lax.all_to_all(outgoing, ('dom', 'sub'), split_axis=0, concat_axis=0, til...  142 us
    pallas_call x1, Pallas kernels, front(): pl.pallas_call(front_kernel, grid=(peers // ROW_LISTS,), in_specs=[pl.Blo...  13.4 us
    pallas_call x1, Pallas kernels, inner_aggregate(): pl.pallas_call(inner_kernel, in_specs=[pl.BlockSpec(memory_space=pltpu.SM...  11 us
    pallas_call x1, Pallas kernels, outer_aggregate(): pl.pallas_call(outer_kernel, in_specs=[pl.BlockSpec(memory_space=pltpu.SM...  5.85 us

profile of v3, /device:TPU:1, one launch (start us, length us, event | category | flops | bytes accessed | tf_op | source)
XLA Modules:
  0.0 172.9 jit_solution(6608285757660865648)
XLA Ops:
  0.0 13.4 %front.1 = (bf16[128,128,256]{2,1,0:T(8,128)(2,1)}, bf16[1024,256]{1,0:T(8,128)(2,1)}) custom-call(s32[128,128]{1,0:T(8,128)} %bitcast.9, bf16[602,1024]{1,0:T(8,128)(2,1)} %bitcast.17, bf16[602,256]{1,0:T(8,128)(2,1)} %w_ref.1, s32[8,128]{1,0:T(8,128)} %bitcast.11), custom_call_target="tpu_custom_call" | custom-call | tf_op jit(solution)/shard_map/front/pallas_call | solution.py:59
  13.4 0.0 copy-start
  13.4 0.0 copy-start.1
  13.4 0.0 copy-start.2
  13.4 0.0 copy-start.3
  13.4 0.0 copy-start.4
  13.4 0.0 copy-start.5
  13.4 109.5 %all_to_all.10.arrived_ref = bf16[128,128,256]{2,1,0:T(8,128)(2,1)} all-to-all(bf16[128,128,256]{2,1,0:T(8,128)(2,1)} %get-tuple-element.10), channel_id=1, replica_groups=mesh['dom'=16,'sub'=8] {'dom','sub'}, dimensions={0} | all-to-all | bytes 16777216 | tf_op jit(solution)/shard_map/all_to_all | solution.py:245
  122.9 0.0 copy-done
  122.9 0.0 copy-done.1
  122.9 0.0 copy-done.2
  123.0 0.0 copy-done.3
  123.0 0.0 copy-done.4
  123.0 0.0 copy-done.5
  123.0 0.0 copy-start.6
  123.0 11.0 %inner_aggregate.1 = (bf16[192,256]{1,0:T(8,128)(2,1)S(1)}, bf16[128,48,128]{2,1,0:T(8,128)(2,1)}) custom-call(s32[8,32]{1,0:T(8,128)S(1)} %copy-done.4, s32[128,128]{1,0:T(8,128)S(1)} %bitcast.10, bf16[8,32,128,128]{3,2,1,0:T(8,128)(2,1)} %tiles_ref.3, bf16[8,128,256]{2,1,0:T(8,128)(2,1)S(1)} %bitcast.8, bf16[128,128,256]{2,1,0:T(8,128)(2,1)} %all_to_all.10.arrived_ref, ...), custom_call_target="tpu_custom_call" | custom-call | tf_op jit(solution)/shard_map/inner_aggregate/pallas_call | solution.py:181
  134.0 33.0 %all_to_all.11.arrived_ref = bf16[128,48,128]{2,1,0:T(8,128)(2,1)S(1)} all-to-all(bf16[128,48,128]{2,1,0:T(8,128)(2,1)} %get-tuple-element.12), channel_id=1, replica_groups=mesh['dom'=16,'sub'=8] {'dom','sub'}, dimensions={0} | all-to-all | bytes 3145728 | tf_op jit(solution)/shard_map/all_to_all | solution.py:245
  167.0 0.0 copy-done.6
  167.0 5.8 %outer_aggregate.1 = f32[41,1024]{1,0:T(8,128)} custom-call(s32[8,32]{1,0:T(8,128)S(1)} %copy-done.4, bf16[8,32,128,128]{3,2,1,0:T(8,128)(2,1)} %tiles_ref.3, bf16[192,256]{1,0:T(8,128)(2,1)S(1)} %get-tuple-element.11.stacked_ref, bf16[128,48,128]{2,1,0:T(8,128)(2,1)S(1)} %all_to_all.11.arrived_ref, s32[8,128]{1,0:T(8,128)S(1)} %bitcast.13, f32[1,41]{1,0:T(1,128)S(1)} %bitcast.16), custom_call_target="tpu_custom_call" | custom-call | tf_op jit(solution)/shard_map/outer_aggregate/pallas_call | solution.py:229
Async XLA Ops:
  13.4 109.6 %copy-start = (bf16[1024,256]{1,0:T(8,128)(2,1)S(1)}, bf16[1024,256]{1,0:T(8,128)(2,1)}, u32[]{:S(2)}) copy-start(bf16[1024,256]{1,0:T(8,128)(2,1)} %get-tuple-element.9) | copy-start | bytes 1572868
  13.4 109.6 %copy-start.1 = (s32[1,128,128]{2,1,0:T(8,128)S(1)}, s32[1,128,128]{2,1,0:T(8,128)}, u32[]{:S(2)}) copy-start(s32[1,128,128]{2,1,0:T(8,128)} %param.17) | copy-start | bytes 196612
  13.4 109.6 %copy-start.2 = (s32[1024]{0:T(1024)S(1)}, s32[1024]{0:T(1024)}, u32[]{:S(2)}) copy-start(s32[1024]{0:T(1024)} %param.16) | copy-start | bytes 12292
  13.4 109.6 %copy-start.3 = (bf16[256,41]{0,1:T(8,128)(2,1)S(1)}, bf16[256,41]{0,1:T(8,128)(2,1)}, u32[]{:S(2)}) copy-start(bf16[256,41]{0,1:T(8,128)(2,1)} %param.12) | copy-start | bytes 62980
  13.4 109.6 %copy-start.4 = (s32[8,32]{1,0:T(8,128)S(1)}, s32[8,32]{1,0:T(8,128)}, u32[]{:S(2)}) copy-start(s32[8,32]{1,0:T(8,128)} %cols_ref.3) | copy-start | bytes 3076
  13.4 109.6 %copy-start.5 = (f32[256]{0:T(256)S(1)}, f32[256]{0:T(256)}, u32[]{:S(2)}) copy-start(f32[256]{0:T(256)} %param.11) | copy-start | bytes 3076
  123.0 44.0 %copy-start.6 = (f32[41]{0:T(128)S(1)}, f32[41]{0:T(128)}, u32[]{:S(2)}) copy-start(f32[41]{0:T(128)} %param.13) | copy-start | bytes 496

commit v4 on v3

v4 whole, which is shorter than its diff:
```python
import jax
import jax.numpy as jnp
from jax import lax
from jax.experimental import pallas as pl
from jax.experimental.pallas import tpu as pltpu
from jax.sharding import PartitionSpec as P

BLOCK = 128
ROW_LISTS = 32
SCORE_LISTS = 8
QUARTER = 256
SCORE_UNROLL = 4
NT = (((1,), (1,)), ((), ()))
MIB = 2**20


def whole():
    return pl.BlockSpec(memory_space=pltpu.VMEM)


def in_hbm(array):
    return pltpu.with_memory_space_constraint(array, pltpu.HBM)


def in_vmem(array):
    return pltpu.with_memory_space_constraint(array, pltpu.VMEM)


def anywhere():
    return pl.BlockSpec(memory_space=pltpu.HBM)


def front_kernel(
    lists_ref, features_ref, w_ref, degrees_ref, tiles_ref, sent_ref, own_ref, near_ref, pick_ref, tile_sem
):
    height = own_ref.shape[0]
    fetch = pltpu.make_async_copy(tiles_ref, near_ref, tile_sem.at[0])

    @pl.when(pl.program_id(0) == 0)
    def _():
        fetch.start()
        inv = lax.rsqrt(degrees_ref[...].astype(jnp.float32)).T
        for r in range(height // BLOCK):
            part = lax.dot_general(
                features_ref[:, r * BLOCK : (r + 1) * BLOCK],
                w_ref[...],
                (((0,), (0,)), ((), ())),
                preferred_element_type=jnp.float32,
            )
            own_ref[r * BLOCK : (r + 1) * BLOCK] = (part * inv[:, r : r + 1]).astype(jnp.bfloat16)

    by_slot = lists_ref[...].T
    row_of_lane = lax.broadcasted_iota(jnp.int32, (BLOCK, height), 1)
    for p in range(ROW_LISTS):
        pick_ref[p * BLOCK : (p + 1) * BLOCK] = (
            (by_slot[:, p : p + 1] == row_of_lane).astype(jnp.float32).astype(jnp.bfloat16)
        )
    rows = jnp.dot(pick_ref[...], own_ref[...], preferred_element_type=jnp.float32)
    sent_ref[...] = rows.astype(jnp.bfloat16).reshape(sent_ref.shape)

    @pl.when(pl.program_id(0) == pl.num_programs(0) - 1)
    def _():
        fetch.wait()


def front(lists, features_t, w_inner, degrees, tiles):
    peers = lists.shape[0]
    height = features_t.shape[1]
    width = w_inner.shape[1]
    return pl.pallas_call(
        front_kernel,
        grid=(peers // ROW_LISTS,),
        in_specs=[
            pl.BlockSpec((ROW_LISTS, BLOCK), lambda g: (g, 0)),
            pl.BlockSpec(features_t.shape, lambda g: (0, 0)),
            pl.BlockSpec(w_inner.shape, lambda g: (0, 0)),
            pl.BlockSpec(degrees.shape, lambda g: (0, 0)),
            pl.BlockSpec(memory_space=pl.ANY),
        ],
        out_specs=[
            pl.BlockSpec((ROW_LISTS, BLOCK, width), lambda g: (g, 0, 0)),
            pl.BlockSpec((height, width), lambda g: (0, 0)),
            pl.BlockSpec(memory_space=pl.ANY),
        ],
        out_shape=[
            pltpu.HBM((peers, BLOCK, width), jnp.bfloat16),
            jax.ShapeDtypeStruct((height, width), jnp.bfloat16),
            pltpu.VMEM(tiles.shape, tiles.dtype),
        ],
        scratch_shapes=[
            pltpu.VMEM((ROW_LISTS * BLOCK, height), jnp.bfloat16),
            pltpu.SemaphoreType.DMA((1,)),
        ],
        compiler_params=pltpu.CompilerParams(vmem_limit_bytes=28 * MIB),
        name="front",
    )(in_hbm(lists), in_hbm(features_t), in_hbm(w_inner), in_hbm(degrees), in_hbm(tiles))


def inner_kernel(
    cols_ref,
    lists_ref,
    tiles_ref,
    own_ref,
    arrived_ref,
    degrees_ref,
    bias_ref,
    w_ref,
    stacked_ref,
    sent_ref,
    hidden,
    outgoing,
    sent_sems,
):
    row_blocks, count = tiles_ref.shape[:2]
    own_blocks, peers = own_ref.shape[0], arrived_ref.shape[0]
    padded = outgoing.shape[1]
    classes = w_ref.shape[0]
    quarters = stacked_ref.shape[0] // padded
    steps = peers // SCORE_LISTS

    def block(c):
        near = own_ref[jnp.minimum(c, own_blocks - 1)]
        far = arrived_ref[jnp.maximum(c - own_blocks, 0)]
        return jnp.where(c < own_blocks, near, far)

    def list_row(g):
        rows = lists_ref[pl.ds(pl.multiple_of(g * SCORE_LISTS, SCORE_LISTS), SCORE_LISTS)]
        return jnp.concatenate([rows[k : k + 1] for k in range(SCORE_LISTS)], axis=1)

    row_of_sublane = lax.broadcasted_iota(jnp.int32, (QUARTER, SCORE_LISTS * BLOCK), 0)

    inv = lax.rsqrt(degrees_ref[...].astype(jnp.float32)).T
    for r in range(row_blocks):
        left = jnp.concatenate([tiles_ref[r, t] for t in range(count)], axis=1)
        right = jnp.concatenate([block(cols_ref[r, t]) for t in range(count)], axis=0)
        total = jnp.dot(left, right, preferred_element_type=jnp.float32)
        scale = inv[:, r : r + 1]
        row = scale * jnp.maximum(scale * total + bias_ref[...], 0.0)
        hidden[r * BLOCK : (r + 1) * BLOCK] = row.astype(jnp.bfloat16)

    scores = lax.dot_general(w_ref[...], hidden[...], NT, preferred_element_type=jnp.float32)
    scores = jnp.concatenate([scores, jnp.zeros((padded - classes, scores.shape[1]), jnp.float32)], axis=0)
    scores = scores.astype(jnp.bfloat16)
    for q in range(quarters):
        stacked_ref[q * padded : (q + 1) * padded] = scores[:, q * QUARTER : (q + 1) * QUARTER]

    def send(h):
        part = pl.ds(h * SCORE_UNROLL * SCORE_LISTS, SCORE_UNROLL * SCORE_LISTS)
        return pltpu.make_async_copy(outgoing.at[part], sent_ref.at[part], sent_sems.at[h])

    @pl.loop(0, steps // SCORE_UNROLL)
    def _(h):
        for u in range(SCORE_UNROLL):
            g = h * SCORE_UNROLL + u
            quarter = jnp.right_shift(list_row(g), QUARTER.bit_length() - 1)
            low = jnp.bitwise_and(list_row(g), QUARTER - 1)
            pick = (low == row_of_sublane).astype(jnp.float32).astype(jnp.bfloat16)
            every = jnp.dot(stacked_ref[...], pick, preferred_element_type=jnp.float32)
            chosen = jnp.zeros((padded, SCORE_LISTS * BLOCK), jnp.float32)
            for q in range(quarters):
                chosen = jnp.where(quarter == q, every[q * padded : (q + 1) * padded], chosen)
            chosen = chosen.astype(jnp.bfloat16)
            for k in range(SCORE_LISTS):
                outgoing[g * SCORE_LISTS + k] = chosen[:, k * BLOCK : (k + 1) * BLOCK]
        send(h).start()

    for h in range(steps // SCORE_UNROLL):
        send(h).wait()


def inner_aggregate(tile_col, lists, near_tiles, own, arrived, degrees, bias, w_t, padded):
    row_blocks = near_tiles.shape[0]
    peers, _, width = arrived.shape
    height = row_blocks * BLOCK
    return pl.pallas_call(
        inner_kernel,
        in_specs=[pl.BlockSpec(memory_space=pltpu.SMEM), whole()] + [whole()] * 6,
        out_specs=[whole(), anywhere()],
        out_shape=[
            jax.ShapeDtypeStruct((padded * height // QUARTER, QUARTER), jnp.bfloat16),
            pltpu.HBM((peers, padded, BLOCK), jnp.bfloat16),
        ],
        scratch_shapes=[
            pltpu.VMEM((height, width), jnp.bfloat16),
            pltpu.VMEM((peers, padded, BLOCK), jnp.bfloat16),
            pltpu.SemaphoreType.DMA((peers // SCORE_LISTS // SCORE_UNROLL,)),
        ],
        compiler_params=pltpu.CompilerParams(vmem_limit_bytes=20 * MIB),
        name="inner_aggregate",
    )(tile_col, lists, in_vmem(near_tiles), own, in_vmem(arrived), degrees, bias, w_t)


def outer_kernel(cols_ref, tiles_ref, stacked_ref, arrived_ref, degrees_ref, bias_ref, out_ref, space):
    row_blocks, count = tiles_ref.shape[:2]
    padded = arrived_ref.shape[1]
    classes = out_ref.shape[0]
    for r in range(row_blocks):
        quarter, side = divmod(r * BLOCK, QUARTER)
        space[r] = stacked_ref[quarter * padded : (quarter + 1) * padded, side : side + BLOCK]
    space[row_blocks:] = arrived_ref[...]
    inv = lax.rsqrt(degrees_ref[...].astype(jnp.float32))
    bias = bias_ref[...].T
    for r in range(row_blocks):
        left = jnp.concatenate([tiles_ref[r, t] for t in range(count)], axis=1)
        right = jnp.concatenate([space[cols_ref[r, t]] for t in range(count)], axis=1)
        total = lax.dot_general(left, right, NT, preferred_element_type=jnp.float32).T
        out_ref[:, r * BLOCK : (r + 1) * BLOCK] = inv[r : r + 1] * total[:classes] + bias


def outer_aggregate(tile_col, near_tiles, stacked, arrived, degrees, bias):
    row_blocks = near_tiles.shape[0]
    peers, padded, _ = arrived.shape
    return pl.pallas_call(
        outer_kernel,
        in_specs=[pl.BlockSpec(memory_space=pltpu.SMEM)] + [whole()] * 5,
        out_specs=whole(),
        out_shape=jax.ShapeDtypeStruct((bias.shape[1], row_blocks * BLOCK), jnp.float32),
        scratch_shapes=[pltpu.VMEM((row_blocks + peers, padded, BLOCK), jnp.bfloat16)],
        compiler_params=pltpu.CompilerParams(vmem_limit_bytes=16 * MIB),
        name="outer_aggregate",
    )(tile_col, in_vmem(near_tiles), stacked, arrived, degrees, bias)


def exchange(outgoing):
    return lax.all_to_all(outgoing, ("dom", "sub"), split_axis=0, concat_axis=0, tiled=True)


def on_device(
    features, w_inner, bias_inner, w_outer, bias_outer, tiles, tile_col, degrees, send_rows
):
    lists = send_rows[0]
    classes = w_outer.shape[1]
    padded = 16 * ((classes + 15) // 16)
    width = w_inner.shape[1]
    degree_rows = degrees.reshape(-1, BLOCK)
    outgoing, own, near_tiles = front(lists, features.T, w_inner, degree_rows, tiles)
    arrived = exchange(outgoing)
    stacked, outgoing_scores = inner_aggregate(
        tile_col,
        lists,
        near_tiles,
        own.reshape(-1, BLOCK, width),
        arrived,
        degree_rows,
        bias_inner[None, :],
        w_outer.T,
        padded,
    )
    arrived_scores = exchange(outgoing_scores)
    logits_t = outer_aggregate(
        tile_col, near_tiles, stacked, arrived_scores, degree_rows, bias_outer[None, :]
    )
    return logits_t.T


def solution(mesh):
    return jax.shard_map(
        on_device,
        mesh=mesh,
        in_specs=(
            P(("dom", "sub"), None),
            P(),
            P(),
            P(),
            P(),
            P(("dom", "sub"), None, None, None),
            P(("dom", "sub"), None),
            P(("dom", "sub")),
            P(("dom", "sub"), None, None),
        ),
        out_specs=P(("dom", "sub"), None),
        check_vma=False,
    )
```

time: 173 us -> 168 us (0.971)
  Pallas kernels: 30.3 us -> 25.5 us
    pallas_call x1, Pallas kernels: 11 us -> 8.32 us  [inner_aggregate(): pl.pallas_call(inner_kernel, in_specs=[pl.BlockSpec(memory_space=pltpu.SM...]
    pallas_call x1, Pallas kernels: 5.85 us -> 3.76 us  [outer_aggregate(): pl.pallas_call(outer_kernel, in_specs=[pl.BlockSpec(memory_space=pltpu.SM...]
where the time goes in v4:
time: 168 us
  blocking collectives  142 us (85%)
  Pallas kernels  25.5 us (15%)
    all_to_all x2, blocking collectives, exchange(): lax.all_to_all(outgoing, ('dom', 'sub'), split_axis=0, concat_axis=0, til...  142 us
    pallas_call x1, Pallas kernels, front(): pl.pallas_call(front_kernel, grid=(peers // ROW_LISTS,), in_specs=[pl.Blo...  13.4 us
    pallas_call x1, Pallas kernels, inner_aggregate(): pl.pallas_call(inner_kernel, in_specs=[pl.BlockSpec(memory_space=pltpu.SM...  8.32 us
    pallas_call x1, Pallas kernels, outer_aggregate(): pl.pallas_call(outer_kernel, in_specs=[pl.BlockSpec(memory_space=pltpu.SM...  3.76 us

profile of v4, /device:TPU:1, one launch (start us, length us, event | category | flops | bytes accessed | tf_op | source)
XLA Modules:
  0.0 168.0 jit_solution(493621143872817164)
XLA Ops:
  0.0 13.4 %front.1 = (bf16[128,128,256]{2,1,0:T(8,128)(2,1)}, bf16[1024,256]{1,0:T(8,128)(2,1)S(1)}, bf16[8,32,128,128]{3,2,1,0:T(8,128)(2,1)S(1)}) custom-call(s32[128,128]{1,0:T(8,128)} %bitcast.9, bf16[602,1024]{1,0:T(8,128)(2,1)} %bitcast.17, bf16[602,256]{1,0:T(8,128)(2,1)} %w_ref.1, s32[8,128]{1,0:T(8,128)} %bitcast.11, bf16[8,32,128,128]{3,2,1,0:T(8,128)(2,1)} %tiles_ref.1), custom_call_target="tpu_custom_call" | custom-call | tf_op jit(solution)/shard_map/front/pallas_call | solution.py:70
  13.4 0.0 copy-start
  13.5 0.0 copy-start.1
  13.5 0.0 copy-start.2
  13.5 0.0 copy-start.3
  13.5 0.0 copy-start.4
  13.5 109.4 %all_to_all.10.arrived_ref = bf16[128,128,256]{2,1,0:T(8,128)(2,1)S(1)} all-to-all(bf16[128,128,256]{2,1,0:T(8,128)(2,1)} %get-tuple-element.12), channel_id=1, replica_groups=mesh['dom'=16,'sub'=8] {'dom','sub'}, dimensions={0} | all-to-all | bytes 16777216 | tf_op jit(solution)/shard_map/all_to_all | solution.py:225
  122.9 0.0 copy-done
  122.9 0.0 copy-done.1
  122.9 0.0 copy-done.2
  122.9 0.0 copy-done.3
  122.9 0.0 copy-done.4
  123.0 0.0 copy-start.5
  123.0 8.3 %inner_aggregate.1 = (bf16[192,256]{1,0:T(8,128)(2,1)S(1)}, bf16[128,48,128]{2,1,0:T(8,128)(2,1)}) custom-call(s32[8,32]{1,0:T(8,128)S(1)} %copy-done.3, s32[128,128]{1,0:T(8,128)S(1)} %bitcast.10, bf16[8,32,128,128]{3,2,1,0:T(8,128)(2,1)S(1)} %get-tuple-element.10.tiles_ref, bf16[8,128,256]{2,1,0:T(8,128)(2,1)S(1)} %bitcast.8, ...), custom_call_target="tpu_custom_call" | custom-call | tf_op jit(solution)/shard_map/inner_aggregate/pallas_call | solution.py:175
  131.3 33.0 %all_to_all.11.arrived_ref = bf16[128,48,128]{2,1,0:T(8,128)(2,1)S(1)} all-to-all(bf16[128,48,128]{2,1,0:T(8,128)(2,1)} %get-tuple-element.14), channel_id=1, replica_groups=mesh['dom'=16,'sub'=8] {'dom','sub'}, dimensions={0} | all-to-all | bytes 3145728 | tf_op jit(solution)/shard_map/all_to_all | solution.py:225
  164.3 0.0 copy-done.5
  164.3 3.8 %outer_aggregate.1 = f32[41,1024]{1,0:T(8,128)} custom-call(s32[8,32]{1,0:T(8,128)S(1)} %copy-done.3, bf16[8,32,128,128]{3,2,1,0:T(8,128)(2,1)S(1)} %get-tuple-element.10.tiles_ref, bf16[192,256]{1,0:T(8,128)(2,1)S(1)} %get-tuple-element.13.stacked_ref, bf16[128,48,128]{2,1,0:T(8,128)(2,1)S(1)} %all_to_all.11.arrived_ref, s32[8,128]{1,0:T(8,128)S(1)} %bitcast.13, ...), custom_call_target="tpu_custom_call" | custom-call | tf_op jit(solution)/shard_map/outer_aggregate/pallas_call | solution.py:213
Async XLA Ops:
  13.4 109.5 %copy-start = (s32[1,128,128]{2,1,0:T(8,128)S(1)}, s32[1,128,128]{2,1,0:T(8,128)}, u32[]{:S(2)}) copy-start(s32[1,128,128]{2,1,0:T(8,128)} %param.17) | copy-start | bytes 196612
  13.5 109.5 %copy-start.1 = (s32[1024]{0:T(1024)S(1)}, s32[1024]{0:T(1024)}, u32[]{:S(2)}) copy-start(s32[1024]{0:T(1024)} %param.16) | copy-start | bytes 12292
  13.5 109.5 %copy-start.2 = (bf16[256,41]{0,1:T(8,128)(2,1)S(1)}, bf16[256,41]{0,1:T(8,128)(2,1)}, u32[]{:S(2)}) copy-start(bf16[256,41]{0,1:T(8,128)(2,1)} %param.12) | copy-start | bytes 62980
  13.5 109.5 %copy-start.3 = (s32[8,32]{1,0:T(8,128)S(1)}, s32[8,32]{1,0:T(8,128)}, u32[]{:S(2)}) copy-start(s32[8,32]{1,0:T(8,128)} %cols_ref.3) | copy-start | bytes 3076
  13.5 109.5 %copy-start.4 = (f32[256]{0:T(256)S(1)}, f32[256]{0:T(256)}, u32[]{:S(2)}) copy-start(f32[256]{0:T(256)} %param.11) | copy-start | bytes 3076
  123.0 41.3 %copy-start.5 = (f32[41]{0:T(128)S(1)}, f32[41]{0:T(128)}, u32[]{:S(2)}) copy-start(f32[41]{0:T(128)} %param.13) | copy-start | bytes 496

commit v5 on v4

--- a/solution.py
+++ b/solution.py
@@ -127,7 +127,9 @@
         rows = lists_ref[pl.ds(pl.multiple_of(g * SCORE_LISTS, SCORE_LISTS), SCORE_LISTS)]
         return jnp.concatenate([rows[k : k + 1] for k in range(SCORE_LISTS)], axis=1)
 
-    row_of_sublane = lax.broadcasted_iota(jnp.int32, (QUARTER, SCORE_LISTS * BLOCK), 0)
+    row_of_sublane = lax.broadcasted_iota(jnp.int16, (QUARTER, SCORE_LISTS * BLOCK), 0)
+    one = jnp.ones(row_of_sublane.shape, jnp.bfloat16)
+    zero = jnp.zeros(row_of_sublane.shape, jnp.bfloat16)
 
     inv = lax.rsqrt(degrees_ref[...].astype(jnp.float32)).T
     for r in range(row_blocks):
@@ -154,7 +156,8 @@
             g = h * SCORE_UNROLL + u
             quarter = jnp.right_shift(list_row(g), QUARTER.bit_length() - 1)
             low = jnp.bitwise_and(list_row(g), QUARTER - 1)
-            pick = (low == row_of_sublane).astype(jnp.float32).astype(jnp.bfloat16)
+            near_row = jnp.broadcast_to(low, row_of_sublane.shape).astype(jnp.int16) == row_of_sublane
+            pick = jnp.where(near_row, one, zero)
             every = jnp.dot(stacked_ref[...], pick, preferred_element_type=jnp.float32)
             chosen = jnp.zeros((padded, SCORE_LISTS * BLOCK), jnp.float32)
             for q in range(quarters):

time: 168 us -> 167 us (level)
  no operation moved by 1% of the time
where the time goes in v5:
time: 167 us
  blocking collectives  142 us (85%)
  Pallas kernels  24.4 us (15%)
    all_to_all x2, blocking collectives, exchange(): lax.all_to_all(outgoing, ('dom', 'sub'), split_axis=0, concat_axis=0, til...  142 us
    pallas_call x1, Pallas kernels, front(): pl.pallas_call(front_kernel, grid=(peers // ROW_LISTS,), in_specs=[pl.Blo...  13.4 us
    pallas_call x1, Pallas kernels, inner_aggregate(): pl.pallas_call(inner_kernel, in_specs=[pl.BlockSpec(memory_space=pltpu.SM...  7.19 us
    pallas_call x1, Pallas kernels, outer_aggregate(): pl.pallas_call(outer_kernel, in_specs=[pl.BlockSpec(memory_space=pltpu.SM...  3.76 us

profile of v5, /device:TPU:1, one launch (start us, length us, event | category | flops | bytes accessed | tf_op | source)
XLA Modules:
  0.0 166.9 jit_solution(6463520748232760074)
XLA Ops:
  0.0 13.4 %front.1 = (bf16[128,128,256]{2,1,0:T(8,128)(2,1)}, bf16[1024,256]{1,0:T(8,128)(2,1)S(1)}, bf16[8,32,128,128]{3,2,1,0:T(8,128)(2,1)S(1)}) custom-call(s32[128,128]{1,0:T(8,128)} %bitcast.9, bf16[602,1024]{1,0:T(8,128)(2,1)} %bitcast.17, bf16[602,256]{1,0:T(8,128)(2,1)} %w_ref.1, s32[8,128]{1,0:T(8,128)} %bitcast.11, bf16[8,32,128,128]{3,2,1,0:T(8,128)(2,1)} %tiles_ref.1), custom_call_target="tpu_custom_call" | custom-call | tf_op jit(solution)/shard_map/front/pallas_call | solution.py:70
  13.4 0.0 copy-start
  13.5 0.0 copy-start.1
  13.5 0.0 copy-start.2
  13.5 0.0 copy-start.3
  13.5 0.0 copy-start.4
  13.5 109.4 %all_to_all.10.arrived_ref = bf16[128,128,256]{2,1,0:T(8,128)(2,1)S(1)} all-to-all(bf16[128,128,256]{2,1,0:T(8,128)(2,1)} %get-tuple-element.12), channel_id=1, replica_groups=mesh['dom'=16,'sub'=8] {'dom','sub'}, dimensions={0} | all-to-all | bytes 16777216 | tf_op jit(solution)/shard_map/all_to_all | solution.py:228
  122.9 0.0 copy-done
  122.9 0.0 copy-done.1
  122.9 0.0 copy-done.2
  122.9 0.0 copy-done.3
  122.9 0.0 copy-done.4
  123.0 0.0 copy-start.5
  123.0 7.2 %inner_aggregate.1 = (bf16[192,256]{1,0:T(8,128)(2,1)S(1)}, bf16[128,48,128]{2,1,0:T(8,128)(2,1)}) custom-call(s32[8,32]{1,0:T(8,128)S(1)} %copy-done.3, s32[128,128]{1,0:T(8,128)S(1)} %bitcast.10, bf16[8,32,128,128]{3,2,1,0:T(8,128)(2,1)S(1)} %get-tuple-element.10.tiles_ref, bf16[8,128,256]{2,1,0:T(8,128)(2,1)S(1)} %bitcast.8, ...), custom_call_target="tpu_custom_call" | custom-call | tf_op jit(solution)/shard_map/inner_aggregate/pallas_call | solution.py:178
  130.2 33.0 %all_to_all.11.arrived_ref = bf16[128,48,128]{2,1,0:T(8,128)(2,1)S(1)} all-to-all(bf16[128,48,128]{2,1,0:T(8,128)(2,1)} %get-tuple-element.14), channel_id=1, replica_groups=mesh['dom'=16,'sub'=8] {'dom','sub'}, dimensions={0} | all-to-all | bytes 3145728 | tf_op jit(solution)/shard_map/all_to_all | solution.py:228
  163.1 0.0 copy-done.5
  163.1 3.8 %outer_aggregate.1 = f32[41,1024]{1,0:T(8,128)} custom-call(s32[8,32]{1,0:T(8,128)S(1)} %copy-done.3, bf16[8,32,128,128]{3,2,1,0:T(8,128)(2,1)S(1)} %get-tuple-element.10.tiles_ref, bf16[192,256]{1,0:T(8,128)(2,1)S(1)} %get-tuple-element.13.stacked_ref, bf16[128,48,128]{2,1,0:T(8,128)(2,1)S(1)} %all_to_all.11.arrived_ref, s32[8,128]{1,0:T(8,128)S(1)} %bitcast.13, ...), custom_call_target="tpu_custom_call" | custom-call | tf_op jit(solution)/shard_map/outer_aggregate/pallas_call | solution.py:216
Async XLA Ops:
  13.4 109.5 %copy-start = (s32[1,128,128]{2,1,0:T(8,128)S(1)}, s32[1,128,128]{2,1,0:T(8,128)}, u32[]{:S(2)}) copy-start(s32[1,128,128]{2,1,0:T(8,128)} %param.17) | copy-start | bytes 196612
  13.5 109.5 %copy-start.1 = (s32[1024]{0:T(1024)S(1)}, s32[1024]{0:T(1024)}, u32[]{:S(2)}) copy-start(s32[1024]{0:T(1024)} %param.16) | copy-start | bytes 12292
  13.5 109.5 %copy-start.2 = (bf16[256,41]{0,1:T(8,128)(2,1)S(1)}, bf16[256,41]{0,1:T(8,128)(2,1)}, u32[]{:S(2)}) copy-start(bf16[256,41]{0,1:T(8,128)(2,1)} %param.12) | copy-start | bytes 62980
  13.5 109.5 %copy-start.3 = (s32[8,32]{1,0:T(8,128)S(1)}, s32[8,32]{1,0:T(8,128)}, u32[]{:S(2)}) copy-start(s32[8,32]{1,0:T(8,128)} %cols_ref.3) | copy-start | bytes 3076
  13.5 109.5 %copy-start.4 = (f32[256]{0:T(256)S(1)}, f32[256]{0:T(256)}, u32[]{:S(2)}) copy-start(f32[256]{0:T(256)} %param.11) | copy-start | bytes 3076
  123.0 40.2 %copy-start.5 = (f32[41]{0:T(128)S(1)}, f32[41]{0:T(128)}, u32[]{:S(2)}) copy-start(f32[41]{0:T(128)} %param.13) | copy-start | bytes 496

commit v6 on v5

--- a/solution.py
+++ b/solution.py
@@ -83,7 +83,7 @@
             pl.BlockSpec(memory_space=pl.ANY),
         ],
         out_shape=[
-            pltpu.HBM((peers, BLOCK, width), jnp.bfloat16),
+            pltpu.VMEM((peers, BLOCK, width), jnp.bfloat16),
             jax.ShapeDtypeStruct((height, width), jnp.bfloat16),
             pltpu.VMEM(tiles.shape, tiles.dtype),
         ],
@@ -106,10 +106,8 @@
     bias_ref,
     w_ref,
     stacked_ref,
-    sent_ref,
+    outgoing,
     hidden,
-    outgoing,
-    sent_sems,
 ):
     row_blocks, count = tiles_ref.shape[:2]
     own_blocks, peers = own_ref.shape[0], arrived_ref.shape[0]
@@ -145,10 +143,6 @@
     scores = scores.astype(jnp.bfloat16)
     for q in range(quarters):
         stacked_ref[q * padded : (q + 1) * padded] = scores[:, q * QUARTER : (q + 1) * QUARTER]
-
-    def send(h):
-        part = pl.ds(h * SCORE_UNROLL * SCORE_LISTS, SCORE_UNROLL * SCORE_LISTS)
-        return pltpu.make_async_copy(outgoing.at[part], sent_ref.at[part], sent_sems.at[h])
 
     @pl.loop(0, steps // SCORE_UNROLL)
     def _(h):
@@ -165,10 +159,6 @@
             chosen = chosen.astype(jnp.bfloat16)
             for k in range(SCORE_LISTS):
                 outgoing[g * SCORE_LISTS + k] = chosen[:, k * BLOCK : (k + 1) * BLOCK]
-        send(h).start()
-
-    for h in range(steps // SCORE_UNROLL):
-        send(h).wait()
 
 
 def inner_aggregate(tile_col, lists, near_tiles, own, arrived, degrees, bias, w_t, padded):
@@ -178,15 +168,13 @@
     return pl.pallas_call(
         inner_kernel,
         in_specs=[pl.BlockSpec(memory_space=pltpu.SMEM), whole()] + [whole()] * 6,
-        out_specs=[whole(), anywhere()],
+        out_specs=[whole(), whole()],
         out_shape=[
             jax.ShapeDtypeStruct((padded * height // QUARTER, QUARTER), jnp.bfloat16),
-            pltpu.HBM((peers, padded, BLOCK), jnp.bfloat16),
+            pltpu.VMEM((peers, padded, BLOCK), jnp.bfloat16),
         ],
         scratch_shapes=[
             pltpu.VMEM((height, width), jnp.bfloat16),
-            pltpu.VMEM((peers, padded, BLOCK), jnp.bfloat16),
-            pltpu.SemaphoreType.DMA((peers // SCORE_LISTS // SCORE_UNROLL,)),
         ],
         compiler_params=pltpu.CompilerParams(vmem_limit_bytes=20 * MIB),
         name="inner_aggregate",

time: 167 us -> 165 us (0.988)
  Pallas kernels: 24.4 us -> 22.2 us
where the time goes in v6:
time: 165 us; the launch traced here: 164 us
  blocking collectives  142 us (86%)
  Pallas kernels  22.2 us (13%)
    all_to_all x2, blocking collectives, exchange(): lax.all_to_all(outgoing, ('dom', 'sub'), split_axis=0, concat_axis=0, til...  142 us
    pallas_call x1, Pallas kernels, front(): pl.pallas_call(front_kernel, grid=(peers // ROW_LISTS,), in_specs=[pl.Blo...  12.1 us
    pallas_call x1, Pallas kernels, inner_aggregate(): pl.pallas_call(inner_kernel, in_specs=[pl.BlockSpec(memory_space=pltpu.SM...  6.39 us
    pallas_call x1, Pallas kernels, outer_aggregate(): pl.pallas_call(outer_kernel, in_specs=[pl.BlockSpec(memory_space=pltpu.SM...  3.76 us

profile of v6, /device:TPU:1, one launch (start us, length us, event | category | flops | bytes accessed | tf_op | source)
XLA Modules:
  0.0 164.3 jit_solution(5676511708563142969)
XLA Ops:
  0.0 12.1 %front.1 = (bf16[128,128,256]{2,1,0:T(8,128)(2,1)S(1)}, bf16[1024,256]{1,0:T(8,128)(2,1)S(1)}, bf16[8,32,128,128]{3,2,1,0:T(8,128)(2,1)S(1)}) custom-call(s32[128,128]{1,0:T(8,128)} %bitcast.9, bf16[602,1024]{1,0:T(8,128)(2,1)} %bitcast.17, bf16[602,256]{1,0:T(8,128)(2,1)} %w_ref.1, s32[8,128]{1,0:T(8,128)} %bitcast.11, bf16[8,32,128,128]{3,2,1,0:T(8,128)(2,1)} %tiles_ref.1), custom_call_target="tpu_custom_call" | custom-call | tf_op jit(solution)/shard_map/front/pallas_call | solution.py:70
  12.1 0.0 copy-start
  12.1 0.0 copy-start.1
  12.1 0.0 copy-start.2
  12.1 0.0 copy-start.3
  12.1 0.0 copy-start.4
  12.2 109.2 %all_to_all.10.arrived_ref = bf16[128,128,256]{2,1,0:T(8,128)(2,1)S(1)} all-to-all(bf16[128,128,256]{2,1,0:T(8,128)(2,1)S(1)} %get-tuple-element.12), channel_id=1, replica_groups=mesh['dom'=16,'sub'=8] {'dom','sub'}, dimensions={0} | all-to-all | bytes 16777216 | tf_op jit(solution)/shard_map/all_to_all | solution.py:216
  121.3 0.0 copy-done
  121.4 0.0 copy-done.1
  121.4 0.0 copy-done.2
  121.4 0.0 copy-done.3
  121.4 0.0 copy-done.4
  121.4 0.0 copy-start.5
  121.4 6.4 %inner_aggregate.1 = (bf16[192,256]{1,0:T(8,128)(2,1)S(1)}, bf16[128,48,128]{2,1,0:T(8,128)(2,1)S(1)}) custom-call(s32[8,32]{1,0:T(8,128)S(1)} %copy-done.3, s32[128,128]{1,0:T(8,128)S(1)} %bitcast.10, bf16[8,32,128,128]{3,2,1,0:T(8,128)(2,1)S(1)} %get-tuple-element.10.tiles_ref, bf16[8,128,256]{2,1,0:T(8,128)(2,1)S(1)} %bitcast.8, ...), custom_call_target="tpu_custom_call" | custom-call | tf_op jit(solution)/shard_map/inner_aggregate/pallas_call | solution.py:168
  127.8 32.8 %all_to_all.11.arrived_ref = bf16[128,48,128]{2,1,0:T(8,128)(2,1)S(1)} all-to-all(bf16[128,48,128]{2,1,0:T(8,128)(2,1)S(1)} %get-tuple-element.14), channel_id=1, replica_groups=mesh['dom'=16,'sub'=8] {'dom','sub'}, dimensions={0} | all-to-all | bytes 3145728 | tf_op jit(solution)/shard_map/all_to_all | solution.py:216
  160.6 0.0 copy-done.5
  160.6 3.8 %outer_aggregate.1 = f32[41,1024]{1,0:T(8,128)} custom-call(s32[8,32]{1,0:T(8,128)S(1)} %copy-done.3, bf16[8,32,128,128]{3,2,1,0:T(8,128)(2,1)S(1)} %get-tuple-element.10.tiles_ref, bf16[192,256]{1,0:T(8,128)(2,1)S(1)} %get-tuple-element.13.stacked_ref, bf16[128,48,128]{2,1,0:T(8,128)(2,1)S(1)} %all_to_all.11.arrived_ref, s32[8,128]{1,0:T(8,128)S(1)} %bitcast.13, ...), custom_call_target="tpu_custom_call" | custom-call | tf_op jit(solution)/shard_map/outer_aggregate/pallas_call | solution.py:204
Async XLA Ops:
  12.1 109.3 %copy-start = (s32[1,128,128]{2,1,0:T(8,128)S(1)}, s32[1,128,128]{2,1,0:T(8,128)}, u32[]{:S(2)}) copy-start(s32[1,128,128]{2,1,0:T(8,128)} %param.17) | copy-start | bytes 196612
  12.1 109.2 %copy-start.1 = (s32[1024]{0:T(1024)S(1)}, s32[1024]{0:T(1024)}, u32[]{:S(2)}) copy-start(s32[1024]{0:T(1024)} %param.16) | copy-start | bytes 12292
  12.1 109.2 %copy-start.2 = (bf16[256,41]{0,1:T(8,128)(2,1)S(1)}, bf16[256,41]{0,1:T(8,128)(2,1)}, u32[]{:S(2)}) copy-start(bf16[256,41]{0,1:T(8,128)(2,1)} %param.12) | copy-start | bytes 62980
  12.1 109.2 %copy-start.3 = (s32[8,32]{1,0:T(8,128)S(1)}, s32[8,32]{1,0:T(8,128)}, u32[]{:S(2)}) copy-start(s32[8,32]{1,0:T(8,128)} %cols_ref.3) | copy-start | bytes 3076
  12.1 109.2 %copy-start.4 = (f32[256]{0:T(256)S(1)}, f32[256]{0:T(256)}, u32[]{:S(2)}) copy-start(f32[256]{0:T(256)} %param.11) | copy-start | bytes 3076
  121.4 39.2 %copy-start.5 = (f32[41]{0:T(128)S(1)}, f32[41]{0:T(128)}, u32[]{:S(2)}) copy-start(f32[41]{0:T(128)} %param.13) | copy-start | bytes 496

commit v7 on v6

--- a/solution.py
+++ b/solution.py
@@ -6,7 +6,7 @@
 from jax.sharding import PartitionSpec as P
 
 BLOCK = 128
-ROW_LISTS = 32
+ROW_LISTS = 64
 SCORE_LISTS = 8
 QUARTER = 256
 SCORE_UNROLL = 4
@@ -35,32 +35,31 @@
 ):
     height = own_ref.shape[0]
     fetch = pltpu.make_async_copy(tiles_ref, near_ref, tile_sem.at[0])
-
-    @pl.when(pl.program_id(0) == 0)
-    def _():
-        fetch.start()
-        inv = lax.rsqrt(degrees_ref[...].astype(jnp.float32)).T
-        for r in range(height // BLOCK):
-            part = lax.dot_general(
-                features_ref[:, r * BLOCK : (r + 1) * BLOCK],
-                w_ref[...],
-                (((0,), (0,)), ((), ())),
-                preferred_element_type=jnp.float32,
+    fetch.start()
+    inv = lax.rsqrt(degrees_ref[...].astype(jnp.float32)).T
+    for r in range(height // BLOCK):
+        part = lax.dot_general(
+            features_ref[:, r * BLOCK : (r + 1) * BLOCK],
+            w_ref[...],
+            (((0,), (0,)), ((), ())),
+            preferred_element_type=jnp.float32,
+        )
+        own_ref[r * BLOCK : (r + 1) * BLOCK] = (part * inv[:, r : r + 1]).astype(jnp.bfloat16)
+
+    row_of_lane = lax.broadcasted_iota(jnp.int32, (BLOCK, height), 1)
+
+    @pl.loop(0, sent_ref.shape[0] // ROW_LISTS)
+    def _(g):
+        here = pl.ds(pl.multiple_of(g * ROW_LISTS, ROW_LISTS), ROW_LISTS)
+        by_slot = lists_ref[here].T
+        for p in range(ROW_LISTS):
+            pick_ref[p * BLOCK : (p + 1) * BLOCK] = (
+                (by_slot[:, p : p + 1] == row_of_lane).astype(jnp.float32).astype(jnp.bfloat16)
             )
-            own_ref[r * BLOCK : (r + 1) * BLOCK] = (part * inv[:, r : r + 1]).astype(jnp.bfloat16)
-
-    by_slot = lists_ref[...].T
-    row_of_lane = lax.broadcasted_iota(jnp.int32, (BLOCK, height), 1)
-    for p in range(ROW_LISTS):
-        pick_ref[p * BLOCK : (p + 1) * BLOCK] = (
-            (by_slot[:, p : p + 1] == row_of_lane).astype(jnp.float32).astype(jnp.bfloat16)
-        )
-    rows = jnp.dot(pick_ref[...], own_ref[...], preferred_element_type=jnp.float32)
-    sent_ref[...] = rows.astype(jnp.bfloat16).reshape(sent_ref.shape)
-
-    @pl.when(pl.program_id(0) == pl.num_programs(0) - 1)
-    def _():
-        fetch.wait()
+        rows = jnp.dot(pick_ref[...], own_ref[...], preferred_element_type=jnp.float32)
+        sent_ref[here] = rows.astype(jnp.bfloat16).reshape(ROW_LISTS, BLOCK, rows.shape[1])
+
+    fetch.wait()
 
 
 def front(lists, features_t, w_inner, degrees, tiles):
@@ -69,19 +68,8 @@
     width = w_inner.shape[1]
     return pl.pallas_call(
         front_kernel,
-        grid=(peers // ROW_LISTS,),
-        in_specs=[
-            pl.BlockSpec((ROW_LISTS, BLOCK), lambda g: (g, 0)),
-            pl.BlockSpec(features_t.shape, lambda g: (0, 0)),
-            pl.BlockSpec(w_inner.shape, lambda g: (0, 0)),
-            pl.BlockSpec(degrees.shape, lambda g: (0, 0)),
-            pl.BlockSpec(memory_space=pl.ANY),
-        ],
-        out_specs=[
-            pl.BlockSpec((ROW_LISTS, BLOCK, width), lambda g: (g, 0, 0)),
-            pl.BlockSpec((height, width), lambda g: (0, 0)),
-            pl.BlockSpec(memory_space=pl.ANY),
-        ],
+        in_specs=[whole()] * 4 + [anywhere()],
+        out_specs=[whole(), whole(), pl.BlockSpec(memory_space=pl.ANY)],
         out_shape=[
             pltpu.VMEM((peers, BLOCK, width), jnp.bfloat16),
             jax.ShapeDtypeStruct((height, width), jnp.bfloat16),
@@ -91,7 +79,7 @@
             pltpu.VMEM((ROW_LISTS * BLOCK, height), jnp.bfloat16),
             pltpu.SemaphoreType.DMA((1,)),
         ],
-        compiler_params=pltpu.CompilerParams(vmem_limit_bytes=28 * MIB),
+        compiler_params=pltpu.CompilerParams(vmem_limit_bytes=36 * MIB),
         name="front",
     )(in_hbm(lists), in_hbm(features_t), in_hbm(w_inner), in_hbm(degrees), in_hbm(tiles))
 

time: 165 us -> 164 us (level)
  no operation moved by 1% of the time
where the time goes in v7:
time: 164 us
  blocking collectives  142 us (87%)
  Pallas kernels  21.5 us (13%)
    all_to_all x2, blocking collectives, exchange(): lax.all_to_all(outgoing, ('dom', 'sub'), split_axis=0, concat_axis=0, til...  142 us
    pallas_call x1, Pallas kernels, front(): pl.pallas_call(front_kernel, in_specs=[whole()] * 4 + [anywhere()], out_s...  11.4 us
    pallas_call x1, Pallas kernels, inner_aggregate(): pl.pallas_call(inner_kernel, in_specs=[pl.BlockSpec(memory_space=pltpu.SM...  6.39 us
    pallas_call x1, Pallas kernels, outer_aggregate(): pl.pallas_call(outer_kernel, in_specs=[pl.BlockSpec(memory_space=pltpu.SM...  3.76 us

profile of v7, /device:TPU:1, one launch (start us, length us, event | category | flops | bytes accessed | tf_op | source)
XLA Modules:
  0.0 163.6 jit_solution(18099308653675364490)
XLA Ops:
  0.0 11.4 %front.1 = (bf16[128,128,256]{2,1,0:T(8,128)(2,1)S(1)}, bf16[1024,256]{1,0:T(8,128)(2,1)S(1)}, bf16[8,32,128,128]{3,2,1,0:T(8,128)(2,1)S(1)}) custom-call(s32[128,128]{1,0:T(8,128)} %bitcast.9, bf16[602,1024]{1,0:T(8,128)(2,1)} %bitcast.17, bf16[602,256]{1,0:T(8,128)(2,1)} %w_ref.1, s32[8,128]{1,0:T(8,128)} %bitcast.11, bf16[8,32,128,128]{3,2,1,0:T(8,128)(2,1)} %tiles_ref.1), custom_call_target="tpu_custom_call" | custom-call | tf_op jit(solution)/shard_map/front/pallas_call | solution.py:69
  11.4 0.0 copy-start
  11.4 0.0 copy-start.1
  11.4 0.0 copy-start.2
  11.4 0.0 copy-start.3
  11.4 0.0 copy-start.4
  11.5 109.2 %all_to_all.10.arrived_ref = bf16[128,128,256]{2,1,0:T(8,128)(2,1)S(1)} all-to-all(bf16[128,128,256]{2,1,0:T(8,128)(2,1)S(1)} %get-tuple-element.12), channel_id=1, replica_groups=mesh['dom'=16,'sub'=8] {'dom','sub'}, dimensions={0} | all-to-all | bytes 16777216 | tf_op jit(solution)/shard_map/all_to_all | solution.py:204
  120.7 0.0 copy-done
  120.7 0.0 copy-done.1
  120.7 0.0 copy-done.2
  120.7 0.0 copy-done.3
  120.7 0.0 copy-done.4
  120.7 0.0 copy-start.5
  120.7 6.4 %inner_aggregate.1 = (bf16[192,256]{1,0:T(8,128)(2,1)S(1)}, bf16[128,48,128]{2,1,0:T(8,128)(2,1)S(1)}) custom-call(s32[8,32]{1,0:T(8,128)S(1)} %copy-done.3, s32[128,128]{1,0:T(8,128)S(1)} %bitcast.10, bf16[8,32,128,128]{3,2,1,0:T(8,128)(2,1)S(1)} %get-tuple-element.10.tiles_ref, bf16[8,128,256]{2,1,0:T(8,128)(2,1)S(1)} %bitcast.8, ...), custom_call_target="tpu_custom_call" | custom-call | tf_op jit(solution)/shard_map/inner_aggregate/pallas_call | solution.py:156
  127.1 32.7 %all_to_all.11.arrived_ref = bf16[128,48,128]{2,1,0:T(8,128)(2,1)S(1)} all-to-all(bf16[128,48,128]{2,1,0:T(8,128)(2,1)S(1)} %get-tuple-element.14), channel_id=1, replica_groups=mesh['dom'=16,'sub'=8] {'dom','sub'}, dimensions={0} | all-to-all | bytes 3145728 | tf_op jit(solution)/shard_map/all_to_all | solution.py:204
  159.8 0.0 copy-done.5
  159.8 3.8 %outer_aggregate.1 = f32[41,1024]{1,0:T(8,128)} custom-call(s32[8,32]{1,0:T(8,128)S(1)} %copy-done.3, bf16[8,32,128,128]{3,2,1,0:T(8,128)(2,1)S(1)} %get-tuple-element.10.tiles_ref, bf16[192,256]{1,0:T(8,128)(2,1)S(1)} %get-tuple-element.13.stacked_ref, bf16[128,48,128]{2,1,0:T(8,128)(2,1)S(1)} %all_to_all.11.arrived_ref, s32[8,128]{1,0:T(8,128)S(1)} %bitcast.13, ...), custom_call_target="tpu_custom_call" | custom-call | tf_op jit(solution)/shard_map/outer_aggregate/pallas_call | solution.py:192
Async XLA Ops:
  11.4 109.3 %copy-start = (s32[1,128,128]{2,1,0:T(8,128)S(1)}, s32[1,128,128]{2,1,0:T(8,128)}, u32[]{:S(2)}) copy-start(s32[1,128,128]{2,1,0:T(8,128)} %param.17) | copy-start | bytes 196612
  11.4 109.3 %copy-start.1 = (s32[1024]{0:T(1024)S(1)}, s32[1024]{0:T(1024)}, u32[]{:S(2)}) copy-start(s32[1024]{0:T(1024)} %param.16) | copy-start | bytes 12292
  11.4 109.2 %copy-start.2 = (bf16[256,41]{0,1:T(8,128)(2,1)S(1)}, bf16[256,41]{0,1:T(8,128)(2,1)}, u32[]{:S(2)}) copy-start(bf16[256,41]{0,1:T(8,128)(2,1)} %param.12) | copy-start | bytes 62980
  11.4 109.2 %copy-start.3 = (s32[8,32]{1,0:T(8,128)S(1)}, s32[8,32]{1,0:T(8,128)}, u32[]{:S(2)}) copy-start(s32[8,32]{1,0:T(8,128)} %cols_ref.3) | copy-start | bytes 3076
  11.4 109.2 %copy-start.4 = (f32[256]{0:T(256)S(1)}, f32[256]{0:T(256)}, u32[]{:S(2)}) copy-start(f32[256]{0:T(256)} %param.11) | copy-start | bytes 3076
  120.7 39.1 %copy-start.5 = (f32[41]{0:T(128)S(1)}, f32[41]{0:T(128)}, u32[]{:S(2)}) copy-start(f32[41]{0:T(128)} %param.13) | copy-start | bytes 496
